TPU v7x, 32 devices: a whole 2x2x4 slice. The times are simulated.
32 devices in a mesh: region: 2 (over x), orig: 2 (over core), shel: 8 (over z, y).
Axes of the slice: x: 2, y: 2, z: 4, core: 2. Of those that a mesh axis runs over, the one named last changes fastest.
Arguments:
- anchor_embed: float32 [32, 65536], P(None, ('region', 'orig')), parts along dimension 1, may hold values from -7 to 7
- shelter_embed: float32 [32, 2048], P(None, ('region', 'shel')), parts along dimension 1, may hold values from -7 to 7
- hazard: float32 [2, 2048], P(None, ('region', 'shel')), parts along dimension 1, may hold values from 0 to 1
- shelter_pot: float32 [2, 2048], P(None, ('region', 'shel')), parts along dimension 1, may hold values from -30 to 29
Outputs:
- anchor_pot: float32 [2, 65536], P(None, ('region', 'orig')), parts along dimension 1
- new_shelter_pot: float32 [2, 2048], P(None, ('region', 'shel')), parts along dimension 1
There are 2 independent parts, one for each index of `region`. A program takes and returns all parts, laid end to end along the dimension named above; each array names one. Nothing has to cross between parts.
All inputs are finite; a program needn't handle non-finite values.
Results may differ from a plain program's by a relative error of at most 0.0003.
Values sent between devices are 32-bit elements; how exact they have to be, the bound alone decides.
No kernel may reach another device: no remote copies, remote signals or barrier semaphores. Data moves between devices by JAX's collectives and lax.ppermute only.
A program may use at most 64 MiB of HBM per device.

v0:
```python
import math

import jax
import jax.numpy as jnp
from jax import lax
from jax.sharding import PartitionSpec as P

EPSILON = 0.25


def merged(array, axis, combine):
    everything = jax.tree.map(lambda part: lax.all_gather(part, axis), array)
    first = jax.tree.map(lambda part: part[0], everything)

    def step(k, so_far):
        return combine(so_far, jax.tree.map(lambda part: part[k], everything))

    return lax.fori_loop(1, lax.axis_size(axis), step, first)


def joined(first, second):
    upper = jnp.maximum(first[0], second[0])
    return (upper, first[1] * jnp.exp(first[0] - upper) + second[1] * jnp.exp(second[0] - upper))


def on_device(anchor_embed, shelter_embed, hazard, shelter_pot):
    rows = anchor_embed.shape[1]
    columns = shelter_embed.shape[1]
    scenarios = hazard.shape[0]
    anchors = rows * lax.axis_size("orig")
    shelters = columns * lax.axis_size("shel")
    block = math.gcd(rows, 4096)
    count = rows // block
    ynorm = jnp.sum(shelter_embed * shelter_embed, axis=0)

    def tile_cost(start):
        xblock = lax.dynamic_slice_in_dim(anchor_embed, start, block, 1)
        cross = jnp.dot(
            xblock.T,
            shelter_embed,
            precision=lax.Precision.HIGHEST,
            preferred_element_type=jnp.float32,
        )
        xnorm = jnp.sum(xblock * xblock, axis=0)
        dist = (xnorm[:, None] + ynorm[None, :] - 2.0 * cross) / xblock.shape[0]
        return dist[None, :, :] + hazard[:, None, :]

    def row_step(index, carry):
        tops, totals = carry
        start = index * block
        score = (shelter_pot[:, None, :] - tile_cost(start)) / EPSILON
        top = jnp.max(score, axis=2)
        total = jnp.sum(jnp.exp(score - top[:, :, None]), axis=2)
        tops = lax.dynamic_update_slice_in_dim(tops, top, start, 1)
        totals = lax.dynamic_update_slice_in_dim(totals, total, start, 1)
        return (tops, totals)

    empty = jnp.zeros((scenarios, rows), jnp.float32)
    local_top, local_total = lax.fori_loop(0, count, row_step, (empty, empty))
    upper, summed = merged((local_top, local_total), "shel", joined)
    anchor_pot = -EPSILON * math.log(shelters) - EPSILON * (upper + jnp.log(summed))

    def col_step(index, carry):
        top, total = carry
        start = index * block
        fblock = lax.dynamic_slice_in_dim(anchor_pot, start, block, 1)
        score = (fblock[:, :, None] - tile_cost(start)) / EPSILON
        newtop = jnp.maximum(top, jnp.max(score, axis=1))
        total = total * jnp.exp(top - newtop) + jnp.sum(jnp.exp(score - newtop[:, None, :]), axis=1)
        return (newtop, total)

    start_top = jnp.full((scenarios, columns), -jnp.inf, dtype=jnp.float32)
    start_total = jnp.zeros((scenarios, columns), jnp.float32)
    col_top, col_total = lax.fori_loop(0, count, col_step, (start_top, start_total))
    upper_col = lax.pmax(col_top, "orig")
    summed_col = lax.psum(col_total * jnp.exp(col_top - upper_col), "orig")
    new_shelter_pot = -EPSILON * math.log(anchors) - EPSILON * (upper_col + jnp.log(summed_col))
    return (anchor_pot, new_shelter_pot)


def solution(mesh):
    placed = (
        P(None, ("region", "orig")),
        P(None, ("region", "shel")),
        P(None, ("region", "shel")),
        P(None, ("region", "shel")),
    )
    return jax.shard_map(
        on_device,
        mesh=mesh,
        in_specs=placed,
        out_specs=(P(None, ("region", "orig")), P(None, ("region", "shel"))),
        check_vma=False,
    )
```

profile of v0, /device:TPU:0, one launch (start us, length us, event | category | flops | bytes accessed | tf_op | source)
XLA Modules:
  0.0 196.2 jit_solution(4050596945642052547)
XLA Ops:
  7.2 0.0 all-gather.9.cloned.1.call-start
  7.2 0.7 multiply_reduce_fusion.2
  8.0 39.8 %while.48 = (s32[]{:T(128)}, f32[2,16384]{1,0:T(2,128)S(1)}, f32[2,16384]{1,0:T(2,128)S(1)}, f32[2,128]{1,0:T(2,128)}, f32[32,16384]{1,0:T(8,128)}, /*index=5*/f...) while((s32[]{:T(128)}, f32[2,16384]{1,0:T(2,128)S(1)}, ...), condition=%wide.region_5.0_spmd, body=%wide.region_1.0_spmd.sunk | while | flops 213102592 | bytes 7631591 | solution.py:59
  8.0 0.0 copy-start.4
  8.1 1.1 multiply_reduce_fusion.5
  9.2 5.0 %fusion.29 = f32[4096,128]{1,0:T(8,128)S(1)} fusion(f32[32,128]{1,0:T(8,128)} %get-tuple-element.661, f32[128]{0:T(128)S(1)} %get-tuple-element.660, f32[4096]{0:T(1024)S(1)} %multiply_reduce_fusion.5, f32[32,16384]{1,0:T(8,128)} %get-tuple-element.659, s32[]{:T(128)S(6)} %select_n.32), kind=kOutput, calls=%fused_computation.2.clone.1 | convolution fusion | flops 203423744 | bytes 2654724 | tf_op jit(solution)/shard_map/while/body/eval_jaxpr/dot_general | solution.py:38
  14.2 1.2 fusion.30
  15.3 2.6 %exponential_reduce_fusion.4 = f32[2,4096]{1,0:T(2,128)S(1)} fusion(f32[2,4096]{1,0:T(2,128)S(1)} %fusion.30, f32[2,128]{1,0:T(2,128)S(1)} %copy-done.4, f32[4096,128]{1,0:T(8,128)S(1)} %fusion.29, f32[2,128]{1,0:T(2,128)S(1)} %copy-done.6), kind=kLoop, calls=%fused_computation.3.clone.1 | loop fusion | flops 5234688 | bytes 2164736 | tf_op jit(solution)/shard_map/while/body/eval_jaxpr/reduce_sum | solution.py:53
  18.0 0.0 copy-start.4
  18.0 1.1 multiply_reduce_fusion.5
  19.1 5.0 %fusion.29 = f32[4096,128]{1,0:T(8,128)S(1)} fusion(f32[32,128]{1,0:T(8,128)} %get-tuple-element.661, f32[128]{0:T(128)S(1)} %get-tuple-element.660, f32[4096]{0:T(1024)S(1)} %multiply_reduce_fusion.5, f32[32,16384]{1,0:T(8,128)} %get-tuple-element.659, s32[]{:T(128)S(6)} %select_n.32), kind=kOutput, calls=%fused_computation.2.clone.1 | convolution fusion | flops 203423744 | bytes 2654724 | tf_op jit(solution)/shard_map/while/body/eval_jaxpr/dot_general | solution.py:38
  24.1 1.2 fusion.30
  25.3 2.6 %exponential_reduce_fusion.4 = f32[2,4096]{1,0:T(2,128)S(1)} fusion(f32[2,4096]{1,0:T(2,128)S(1)} %fusion.30, f32[2,128]{1,0:T(2,128)S(1)} %copy-done.4, f32[4096,128]{1,0:T(8,128)S(1)} %fusion.29, f32[2,128]{1,0:T(2,128)S(1)} %copy-done.6), kind=kLoop, calls=%fused_computation.3.clone.1 | loop fusion | flops 5234688 | bytes 2164736 | tf_op jit(solution)/shard_map/while/body/eval_jaxpr/reduce_sum | solution.py:53
  27.9 0.0 copy-start.4
  27.9 0.0 copy-start.6
  28.0 1.1 multiply_reduce_fusion.5
  29.1 5.0 %fusion.29 = f32[4096,128]{1,0:T(8,128)S(1)} fusion(f32[32,128]{1,0:T(8,128)} %get-tuple-element.661, f32[128]{0:T(128)S(1)} %get-tuple-element.660, f32[4096]{0:T(1024)S(1)} %multiply_reduce_fusion.5, f32[32,16384]{1,0:T(8,128)} %get-tuple-element.659, s32[]{:T(128)S(6)} %select_n.32), kind=kOutput, calls=%fused_computation.2.clone.1 | convolution fusion | flops 203423744 | bytes 2654724 | tf_op jit(solution)/shard_map/while/body/eval_jaxpr/dot_general | solution.py:38
  34.1 1.2 fusion.30
  35.2 2.6 %exponential_reduce_fusion.4 = f32[2,4096]{1,0:T(2,128)S(1)} fusion(f32[2,4096]{1,0:T(2,128)S(1)} %fusion.30, f32[2,128]{1,0:T(2,128)S(1)} %copy-done.4, f32[4096,128]{1,0:T(8,128)S(1)} %fusion.29, f32[2,128]{1,0:T(2,128)S(1)} %copy-done.6), kind=kLoop, calls=%fused_computation.3.clone.1 | loop fusion | flops 5234688 | bytes 2164736 | tf_op jit(solution)/shard_map/while/body/eval_jaxpr/reduce_sum | solution.py:53
  37.9 0.0 copy-start.6
  37.9 1.1 multiply_reduce_fusion.5
  39.0 5.0 %fusion.29 = f32[4096,128]{1,0:T(8,128)S(1)} fusion(f32[32,128]{1,0:T(8,128)} %get-tuple-element.661, f32[128]{0:T(128)S(1)} %get-tuple-element.660, f32[4096]{0:T(1024)S(1)} %multiply_reduce_fusion.5, f32[32,16384]{1,0:T(8,128)} %get-tuple-element.659, s32[]{:T(128)S(6)} %select_n.32), kind=kOutput, calls=%fused_computation.2.clone.1 | convolution fusion | flops 203423744 | bytes 2654724 | tf_op jit(solution)/shard_map/while/body/eval_jaxpr/dot_general | solution.py:38
  44.0 1.2 fusion.30
  45.2 2.6 %exponential_reduce_fusion.4 = f32[2,4096]{1,0:T(2,128)S(1)} fusion(f32[2,4096]{1,0:T(2,128)S(1)} %fusion.30, f32[2,128]{1,0:T(2,128)S(1)} %copy-done.4, f32[4096,128]{1,0:T(8,128)S(1)} %fusion.29, f32[2,128]{1,0:T(2,128)S(1)} %copy-done.6), kind=kLoop, calls=%fused_computation.3.clone.1 | loop fusion | flops 5234688 | bytes 2164736 | tf_op jit(solution)/shard_map/while/body/eval_jaxpr/reduce_sum | solution.py:53
  47.8 0.0 copy-start.2
  47.8 0.6 copy-done.3
  48.5 0.0 all-gather.9.cloned.1.call-update
  48.5 0.2 all-gather.7.cloned.1.call-start
  48.7 0.5 all-gather.7.cloned.1.call-update
  49.3 42.4 %all-gather.9.cloned.1.call-done = f32[8,2,16384]{2,1,0:T(2,128)} async-done(((f32[1,2,16384]{2,1,0:T(2,128)}), f32[8,2,16384]{2,1,0:T(2,128)}) %all-gather.9.cloned.1.call-update) | async-done | bytes 1048592 | tf_op jit(solution)/shard_map/all_gather | solution.py:12
  91.7 0.9 slice_bitcast_fusion
  92.6 40.8 %all-gather.7.cloned.1.call-done = f32[8,2,16384]{2,1,0:T(2,128)} async-done(((f32[1,2,16384]{2,1,0:T(2,128)}), f32[8,2,16384]{2,1,0:T(2,128)}) %all-gather.7.cloned.1.call-update) | async-done | bytes 1048592 | tf_op jit(solution)/shard_map/all_gather | solution.py:12
  133.4 0.9 slice_bitcast_fusion.1
  134.3 0.0 copy-start.5
  134.3 8.5 %while.49 = (s32[]{:T(128)}, f32[2,16384]{1,0:T(2,128)S(1)}, f32[2,16384]{1,0:T(2,128)S(1)}, f32[8,2,16384]{2,1,0:T(2,128)}, f32[8,2,16384]{2,1,0:T(2,128)}, /*index=5*/s32[]{:T(128)}, s32[]{:T(128)}, s32[]{:T(128)}) while((s32[]{:T(128)}, f32[2,16384]{1,0:T(2,128)S(1)}, f32[2,16384]{1,0:T(2,128)S(1)}, f32[8,2,16384]{2,1,0:T(2,128)}, ...), condition=%wide.region_7.0_spmd, body=%wide.region_6.0_spmd.sunk | while | flops 196613 | bytes 786563 | solution.py:18
  134.3 1.2 fusion.31
  135.6 1.2 fusion.31
  136.8 1.2 fusion.31
  138.0 1.2 fusion.31
  139.2 1.2 fusion.31
  140.4 1.2 fusion.31
  141.6 1.2 fusion.31
  142.8 0.1 multiply_subtract_fusion
  143.0 40.8 %while.50 = (s32[]{:T(128)}, f32[2,128]{1,0:T(2,128)S(1)}, f32[2,128]{1,0:T(2,128)S(1)}, f32[2,16384]{1,0:T(2,128)S(1)}, f32[32,16384]{1,0:T(8,128)}, /*index=5*...) while((s32[]{:T(128)}, f32[2,128]{1,0:T(2,128)S(1)}, ...), condition=%wide.region_12.0_spmd.clone, body=%wide.region_8.0_spmd.clone.sunk | while | flops 213120256 | bytes 7536314 | solution.py:74
  143.0 1.1 multiply_reduce_fusion.6
  144.1 4.9 %fusion.34 = f32[4096,128]{1,0:T(8,128)S(1)} fusion(f32[32,128]{1,0:T(8,128)S(1)} %get-tuple-element.721, f32[128]{0:T(128)S(1)} %get-tuple-element.720, f32[4096]{0:T(1024)S(1)} %multiply_reduce_fusion.6, f32[32,16384]{1,0:T(8,128)} %get-tuple-element.719, s32[]{:T(128)S(6)} %select_n.34), kind=kOutput, calls=%fused_computation.18.clone.1 | convolution fusion | flops 203423744 | bytes 2654724 | tf_op jit(solution)/shard_map/while/body/eval_jaxpr/dot_general | solution.py:38
  149.1 2.0 %fusion.35 = f32[2,128]{1,0:T(2,128)S(1)} fusion(f32[2,128]{1,0:T(2,128)S(1)} %get-tuple-element.722, f32[4096,128]{1,0:T(8,128)S(1)} %fusion.34, f32[2,4096]{1,0:T(2,128)S(1)} %constant_dynamic-slice_fusion.2), kind=kLoop, calls=%fused_computation.21.clone.1 | loop fusion | flops 4194048 | bytes 2131968 | tf_op jit(solution)/shard_map/while/body/eval_jaxpr/reduce_max | solution.py:68
  151.1 2.1 %exponential_reduce_fusion.5 = f32[2,128]{1,0:T(2,128)S(1)} fusion(f32[2,128]{1,0:T(2,128)S(1)} %fusion.36, f32[2,128]{1,0:T(2,128)S(1)} %get-tuple-element.722, f32[4096,128]{1,0:T(8,128)S(1)} %fusion.34, f32[2,4096]{1,0:T(2,128)S(1)} %constant_dynamic-slice_fusion.2), kind=kLoop, calls=%fused_computation.19.clone.1 | loop fusion | flops 5242624 | bytes 2132992 | tf_op jit(solution)/shard_map/while/body/eval_jaxpr/reduce_sum | solution.py:69
  153.2 1.1 multiply_reduce_fusion.6
  154.3 4.9 %fusion.34 = f32[4096,128]{1,0:T(8,128)S(1)} fusion(f32[32,128]{1,0:T(8,128)S(1)} %get-tuple-element.721, f32[128]{0:T(128)S(1)} %get-tuple-element.720, f32[4096]{0:T(1024)S(1)} %multiply_reduce_fusion.6, f32[32,16384]{1,0:T(8,128)} %get-tuple-element.719, s32[]{:T(128)S(6)} %select_n.34), kind=kOutput, calls=%fused_computation.18.clone.1 | convolution fusion | flops 203423744 | bytes 2654724 | tf_op jit(solution)/shard_map/while/body/eval_jaxpr/dot_general | solution.py:38
  159.3 2.0 %fusion.35 = f32[2,128]{1,0:T(2,128)S(1)} fusion(f32[2,128]{1,0:T(2,128)S(1)} %get-tuple-element.722, f32[4096,128]{1,0:T(8,128)S(1)} %fusion.34, f32[2,4096]{1,0:T(2,128)S(1)} %constant_dynamic-slice_fusion.2), kind=kLoop, calls=%fused_computation.21.clone.1 | loop fusion | flops 4194048 | bytes 2131968 | tf_op jit(solution)/shard_map/while/body/eval_jaxpr/reduce_max | solution.py:68
  161.3 2.1 %exponential_reduce_fusion.5 = f32[2,128]{1,0:T(2,128)S(1)} fusion(f32[2,128]{1,0:T(2,128)S(1)} %fusion.36, f32[2,128]{1,0:T(2,128)S(1)} %get-tuple-element.722, f32[4096,128]{1,0:T(8,128)S(1)} %fusion.34, f32[2,4096]{1,0:T(2,128)S(1)} %constant_dynamic-slice_fusion.2), kind=kLoop, calls=%fused_computation.19.clone.1 | loop fusion | flops 5242624 | bytes 2132992 | tf_op jit(solution)/shard_map/while/body/eval_jaxpr/reduce_sum | solution.py:69
  163.4 1.1 multiply_reduce_fusion.6
  164.5 4.9 %fusion.34 = f32[4096,128]{1,0:T(8,128)S(1)} fusion(f32[32,128]{1,0:T(8,128)S(1)} %get-tuple-element.721, f32[128]{0:T(128)S(1)} %get-tuple-element.720, f32[4096]{0:T(1024)S(1)} %multiply_reduce_fusion.6, f32[32,16384]{1,0:T(8,128)} %get-tuple-element.719, s32[]{:T(128)S(6)} %select_n.34), kind=kOutput, calls=%fused_computation.18.clone.1 | convolution fusion | flops 203423744 | bytes 2654724 | tf_op jit(solution)/shard_map/while/body/eval_jaxpr/dot_general | solution.py:38
  169.5 2.0 %fusion.35 = f32[2,128]{1,0:T(2,128)S(1)} fusion(f32[2,128]{1,0:T(2,128)S(1)} %get-tuple-element.722, f32[4096,128]{1,0:T(8,128)S(1)} %fusion.34, f32[2,4096]{1,0:T(2,128)S(1)} %constant_dynamic-slice_fusion.2), kind=kLoop, calls=%fused_computation.21.clone.1 | loop fusion | flops 4194048 | bytes 2131968 | tf_op jit(solution)/shard_map/while/body/eval_jaxpr/reduce_max | solution.py:68
  171.5 2.1 %exponential_reduce_fusion.5 = f32[2,128]{1,0:T(2,128)S(1)} fusion(f32[2,128]{1,0:T(2,128)S(1)} %fusion.36, f32[2,128]{1,0:T(2,128)S(1)} %get-tuple-element.722, f32[4096,128]{1,0:T(8,128)S(1)} %fusion.34, f32[2,4096]{1,0:T(2,128)S(1)} %constant_dynamic-slice_fusion.2), kind=kLoop, calls=%fused_computation.19.clone.1 | loop fusion | flops 5242624 | bytes 2132992 | tf_op jit(solution)/shard_map/while/body/eval_jaxpr/reduce_sum | solution.py:69
  173.6 1.1 multiply_reduce_fusion.6
  174.7 4.9 %fusion.34 = f32[4096,128]{1,0:T(8,128)S(1)} fusion(f32[32,128]{1,0:T(8,128)S(1)} %get-tuple-element.721, f32[128]{0:T(128)S(1)} %get-tuple-element.720, f32[4096]{0:T(1024)S(1)} %multiply_reduce_fusion.6, f32[32,16384]{1,0:T(8,128)} %get-tuple-element.719, s32[]{:T(128)S(6)} %select_n.34), kind=kOutput, calls=%fused_computation.18.clone.1 | convolution fusion | flops 203423744 | bytes 2654724 | tf_op jit(solution)/shard_map/while/body/eval_jaxpr/dot_general | solution.py:38
  179.7 2.0 %fusion.35 = f32[2,128]{1,0:T(2,128)S(1)} fusion(f32[2,128]{1,0:T(2,128)S(1)} %get-tuple-element.722, f32[4096,128]{1,0:T(8,128)S(1)} %fusion.34, f32[2,4096]{1,0:T(2,128)S(1)} %constant_dynamic-slice_fusion.2), kind=kLoop, calls=%fused_computation.21.clone.1 | loop fusion | flops 4194048 | bytes 2131968 | tf_op jit(solution)/shard_map/while/body/eval_jaxpr/reduce_max | solution.py:68
  181.7 2.1 %exponential_reduce_fusion.5 = f32[2,128]{1,0:T(2,128)S(1)} fusion(f32[2,128]{1,0:T(2,128)S(1)} %fusion.36, f32[2,128]{1,0:T(2,128)S(1)} %get-tuple-element.722, f32[4096,128]{1,0:T(8,128)S(1)} %fusion.34, f32[2,4096]{1,0:T(2,128)S(1)} %constant_dynamic-slice_fusion.2), kind=kLoop, calls=%fused_computation.19.clone.1 | loop fusion | flops 5242624 | bytes 2132992 | tf_op jit(solution)/shard_map/while/body/eval_jaxpr/reduce_sum | solution.py:69
  183.8 0.0 copy-start.1
  183.8 2.5 %pmax.7 = f32[2,128]{1,0:T(2,128)S(1)} all-reduce(f32[2,128]{1,0:T(2,128)S(1)} %get-tuple-element.419), channel_id=1, replica_groups=mesh['region'=2,'orig'=2,'shel'=8] {'orig'}, use_global_device_ids=true, to_apply=%region_13.0 | all-reduce | flops 256 | bytes 2048 | tf_op jit(solution)/shard_map/pmax | solution.py:75
  186.3 2.5 %psum.7 = f32[2,128]{1,0:T(2,128)S(1)} all-reduce(f32[2,128]{1,0:T(2,128)S(1)} %exponential_multiply_fusion), channel_id=1, replica_groups=mesh['region'=2,'orig'=2,'shel'=8] {'orig'}, use_global_device_ids=true, to_apply=%region_14.0 | all-reduce | flops 256 | bytes 2048 | tf_op jit(solution)/shard_map/psum | solution.py:76
  188.8 0.6 multiply_subtract_fusion.1
  (42 shorter events, 0.4 us)
Async XLA Ops:
  7.2 84.5 %all-gather.9.cloned.1.call-start = ((), (), s32[]{:S(2)}) async-start(), calls=%async_computation.1 | async-start | bytes 1179648 | tf_op jit(solution)/shard_map/all_gather | solution.py:12
  8.0 6.1 %copy-start.4 = (f32[2,128]{1,0:T(2,128)S(1)}, f32[2,128]{1,0:T(2,128)}, u32[]{:S(2)}) copy-start(f32[2,128]{1,0:T(2,128)} %get-tuple-element.662) | copy-start | bytes 3076 | tf_op jit(solution)/shard_map/while
  8.1 6.1 %copy-start.6 = (f32[2,128]{1,0:T(2,128)S(1)}, f32[2,128]{1,0:T(2,128)}, u32[]{:S(2)}) copy-start(f32[2,128]{1,0:T(2,128)} %get-tuple-element.658) | copy-start | bytes 3076 | tf_op jit(solution)/shard_map/while
  18.0 6.1 %copy-start.4 = (f32[2,128]{1,0:T(2,128)S(1)}, f32[2,128]{1,0:T(2,128)}, u32[]{:S(2)}) copy-start(f32[2,128]{1,0:T(2,128)} %get-tuple-element.662) | copy-start | bytes 3076 | tf_op jit(solution)/shard_map/while
  18.0 6.1 %copy-start.6 = (f32[2,128]{1,0:T(2,128)S(1)}, f32[2,128]{1,0:T(2,128)}, u32[]{:S(2)}) copy-start(f32[2,128]{1,0:T(2,128)} %get-tuple-element.658) | copy-start | bytes 3076 | tf_op jit(solution)/shard_map/while
  27.9 6.1 %copy-start.4 = (f32[2,128]{1,0:T(2,128)S(1)}, f32[2,128]{1,0:T(2,128)}, u32[]{:S(2)}) copy-start(f32[2,128]{1,0:T(2,128)} %get-tuple-element.662) | copy-start | bytes 3076 | tf_op jit(solution)/shard_map/while
  27.9 6.1 %copy-start.6 = (f32[2,128]{1,0:T(2,128)S(1)}, f32[2,128]{1,0:T(2,128)}, u32[]{:S(2)}) copy-start(f32[2,128]{1,0:T(2,128)} %get-tuple-element.658) | copy-start | bytes 3076 | tf_op jit(solution)/shard_map/while
  37.9 6.1 %copy-start.4 = (f32[2,128]{1,0:T(2,128)S(1)}, f32[2,128]{1,0:T(2,128)}, u32[]{:S(2)}) copy-start(f32[2,128]{1,0:T(2,128)} %get-tuple-element.662) | copy-start | bytes 3076 | tf_op jit(solution)/shard_map/while
  37.9 6.1 %copy-start.6 = (f32[2,128]{1,0:T(2,128)S(1)}, f32[2,128]{1,0:T(2,128)}, u32[]{:S(2)}) copy-start(f32[2,128]{1,0:T(2,128)} %get-tuple-element.658) | copy-start | bytes 3076 | tf_op jit(solution)/shard_map/while
  47.8 0.7 copy-start.3
  47.8 0.9 copy-start.2
  48.5 84.9 %all-gather.7.cloned.1.call-start = ((), (), s32[]{:S(2)}) async-start(), calls=%async_computation | async-start | bytes 1179648 | tf_op jit(solution)/shard_map/all_gather | solution.py:12
  134.3 8.7 %copy-start = (f32[32,128]{1,0:T(8,128)S(1)}, f32[32,128]{1,0:T(8,128)}, u32[]{:S(2)}) copy-start(f32[32,128]{1,0:T(8,128)} %get-tuple-element.730) | copy-start | bytes 49156
  134.3 8.7 %copy-start.5 = (f32[2,128]{1,0:T(2,128)S(1)}, f32[2,128]{1,0:T(2,128)}, u32[]{:S(2)}) copy-start(f32[2,128]{1,0:T(2,128)} %get-tuple-element.738) | copy-start | bytes 3076
  183.8 5.5 %copy-start.1 = (f32[2,16384]{1,0:T(2,128)}, f32[2,16384]{1,0:T(2,128)S(1)}, u32[]{:S(2)}) copy-start(f32[2,16384]{1,0:T(2,128)S(1)} %get-tuple-element.731) | copy-start | bytes 393220
Sparse Core Ops, SparseCore 0:
  48.6 42.9 all-gather.8
  94.4 38.9 all-gather.6
where the time goes:
time: 197 us; the launch traced here: 196 us
  waiting for transfers between devices  83.7 us (42%)
  other arithmetic  50.2 us (25%)
  matrix products  39.5 us (20%)
  between operations  14.2 us (7%)
  blocking collectives  4.93 us (3%)
  local copies, waits for them, and re-layouts  2.75 us (1%)
    all_gather x2, waiting for transfers between devices, merged(): everything = jax.tree.map(lambda part: lax.all_gather(part, axis), array)  83.2 us
    dot_general x8, matrix products, tile_cost(): jnp.dot(xblock.T, shelter_embed, precision=lax.Precision.HIGHEST, preferr...  39.5 us
    reduce_sum x4, other arithmetic, row_step(): total = jnp.sum(jnp.exp(score - top[:, :, None]), axis=2)  10.4 us
    reduce_sum x8, other arithmetic, tile_cost(): xnorm = jnp.sum(xblock * xblock, axis=0)  8.89 us
    add x7, other arithmetic, joined(): first[1] * jnp.exp(first[0] - upper)  8.37 us
    reduce_sum x4, other arithmetic, col_step(): jnp.sum(jnp.exp(score - newtop[:, None, :]), axis=1)  8.24 us
    reduce_max x4, other arithmetic, col_step(): newtop = jnp.maximum(top, jnp.max(score, axis=1))  8.07 us
    reduce_max x4, other arithmetic, row_step(): top = jnp.max(score, axis=2)  4.74 us
  transfers between devices with their start and end apart: 2, of which 2 were waited for; matrix products, arithmetic and copies ran while one was open for 0% of the time, Pallas kernels for 0%

commit v1 on v0

v1 whole, which is shorter than its diff:
```python
import functools
import math

import jax
import jax.numpy as jnp
from jax import lax
from jax.experimental import pallas as pl
from jax.experimental.pallas import tpu as pltpu
from jax.sharding import PartitionSpec as P

EPSILON = 0.25
SCALE = math.log2(math.e) / EPSILON
SPREAD = 36.0
DEPTH = 256


def three(v):
    a = v.astype(jnp.bfloat16).astype(jnp.float32)
    rest = v - a
    b = rest.astype(jnp.bfloat16).astype(jnp.float32)
    return a, b, (rest - b).astype(jnp.bfloat16).astype(jnp.float32)


def rows_of(values, count):
    width = next(v.shape[1] for v in values if not isinstance(v, float))
    index = lax.broadcasted_iota(jnp.int32, (count, width), 0)
    out = jnp.zeros((count, width), jnp.float32)
    for k, v in enumerate(values):
        out = jnp.where(index == k, v, out)
    return out


def x_side(x):
    emb = x.shape[0]
    x0, x1, x2 = three(x)
    norm = jnp.sum(x * x, axis=0, keepdims=True) * (-SCALE / emb)
    misc = rows_of((*three(norm), 1.0, 1.0, 1.0), DEPTH - 6 * emb)
    return jnp.concatenate([x0, x0, x1, x1, x0, x2, misc], axis=0).astype(jnp.bfloat16)


def gap_of(z, emb):
    h0, h1, f0, f1 = (z[emb + k : emb + k + 1] for k in range(4))
    return SCALE * ((f1 - h1) - (f0 - h0))


def y_side(z, emb):
    y = z[:emb]
    y0, y1, y2 = three(y * (2.0 * SCALE / emb))
    bias = SCALE * (z[emb + 2 : emb + 3] - z[emb : emb + 1]) - jnp.sum(y * y, axis=0, keepdims=True) * (SCALE / emb)
    misc = rows_of((1.0, 1.0, 1.0, *three(bias)), DEPTH - 6 * emb)
    side = jnp.concatenate([y0, y1, y0, y1, y2, y0, misc], axis=0)
    return side.T.astype(jnp.bfloat16)


def across(row):
    return jnp.broadcast_to(row, (128, row.shape[1])).T


def wide(block, width):
    return jnp.concatenate([block] * (width // 128), axis=1)


def score(side, other):
    return lax.dot_general(side, other, (((1,), (0,)), ((), ())), preferred_element_type=jnp.float32)


def row_sums(side_ref, ratio_ref, start, stop, other, state):
    width = other.shape[1]
    columns = side_ref.shape[1]
    per = max(1, 256 // columns)

    def some(b, count, state):
        top, sum0, sum1 = state
        v = score(side_ref[pl.ds(b, count)].reshape(count * columns, DEPTH), other)
        r = wide(ratio_ref[pl.ds(b, count)].reshape(count * columns, 128), width)
        v = v.reshape(count * columns // 8, 8, width)
        new = jnp.max(v, axis=0)
        if top is not None:
            new = jnp.maximum(top, new)
        e = jnp.exp2(v - new)
        add0, add1 = jnp.sum(e, axis=0), jnp.sum(e * r.reshape(v.shape), axis=0)
        if top is None:
            return new, add0, add1
        less = jnp.exp2(top - new)
        return new, sum0 * less + add0, sum1 * less + add1

    count = min(per, stop - start)
    state = some(start, count, state)
    chunks = (stop - start) // count
    if chunks <= 4:
        for k in range(1, chunks):
            state = some(start + k * count, count, state)
        return state
    return lax.fori_loop(1, chunks, lambda k, s: some(start + k * count, count, s), state)


def one_row(state):
    top, sum0, sum1 = state
    high = jnp.max(top, axis=0, keepdims=True)
    less = jnp.exp2(top - high)
    return high, jnp.sum(sum0 * less, axis=0, keepdims=True), jnp.sum(sum1 * less, axis=0, keepdims=True)


def prepare(z_ref, emb, block, side_ref, ratio_ref, slot):
    z = z_ref[block]
    side_ref[slot] = y_side(z, emb)
    ratio_ref[slot] = across(jnp.exp2(jnp.clip(gap_of(z, emb), -SPREAD, SPREAD)))


def fetches(x_hbm, x_ref, sems, tile):
    def fetch(t):
        at = pl.ds(pl.multiple_of(t * tile, tile), tile)
        return pltpu.make_async_copy(x_hbm.at[:, at], x_ref.at[:, at], sems.at[t])

    def begin(t, carry):
        fetch(t).start()
        return carry

    lax.fori_loop(0, x_ref.shape[1] // tile, begin, 0)
    return fetch


def part_kernel(emb, tile, x_hbm, z_ref, stat_ref, x_ref, sems, side_ref, ratio_ref):
    blocks = z_ref.shape[0]
    fetch = fetches(x_hbm, x_ref, sems, tile)
    for b in range(blocks):
        prepare(z_ref, emb, b, side_ref, ratio_ref, b)

    def step(t, carry):
        fetch(t).wait()
        for part in range(0, tile, 256):
            at = pl.ds(pl.multiple_of(t * tile + part, 256), 256)
            state = row_sums(side_ref, ratio_ref, 0, blocks, x_side(x_ref[:, at]), (None, None, None))
            for k, v in enumerate(one_row(state)):
                stat_ref[k : k + 1, at] = v
        return carry

    lax.fori_loop(0, x_ref.shape[1] // tile, step, 0)


def last_kernel(emb, tile, shelters, known, x_hbm, z_ref, *refs):
    stats = refs[: len(known)]
    anchor_ref, column_ref, x_ref, sems, side_ref, ratio_ref, other_ref, lse_ref = refs[len(known) :]
    blocks, _, columns = z_ref.shape
    first = sum(known)
    left = blocks - first
    tiles = x_ref.shape[1] // tile
    f32 = jnp.float32
    fetch = fetches(x_hbm, x_ref, sems, tile)
    for b in range(left):
        prepare(z_ref, emb, first + b, side_ref, ratio_ref, b)
    prepare(z_ref, emb, 0, side_ref, ratio_ref, left)
    spread = lax.fori_loop(0, blocks, lambda b, w: jnp.maximum(w, jnp.max(jnp.abs(gap_of(z_ref[b], emb)))), f32(0.0))
    near = spread <= SPREAD

    def row_step(t, carry):
        fetch(t).wait()
        for part in range(0, tile, 256):
            at = pl.ds(pl.multiple_of(t * tile + part, 256), 256)
            other = x_side(x_ref[:, at])
            other_ref[:, at] = other
            states = [one_row(row_sums(side_ref, ratio_ref, 0, left, other, (None, None, None)))]
            states += [tuple(ref[k : k + 1, at] for k in range(3)) for ref in stats]
            high = functools.reduce(jnp.maximum, [s[0] for s in states])
            less = [jnp.exp2(s[0] - high) for s in states]
            for k in range(2):
                total = sum(s[1 + k] * m for s, m in zip(states, less))
                lse = high + jnp.log2(total)
                lse_ref[k : k + 1, at] = lse
                anchor_ref[k : k + 1, at] = (-EPSILON * math.log(shelters)) - (EPSILON * math.log(2.0)) * lse
        return carry

    lax.fori_loop(0, tiles, row_step, 0)

    def column_step(t, state):
        top, sum0, sum1 = state
        at = pl.ds(pl.multiple_of(t * tile, tile), tile)
        lse = lse_ref[0:1, at]
        weight = jnp.exp2(jnp.clip(lse - lse_ref[1:2, at], -SPREAD, SPREAD))
        v = score(side_ref[left], other_ref[:, at]) - lse
        parts = [slice(k * 128, (k + 1) * 128) for k in range(tile // 128)]
        new = functools.reduce(jnp.maximum, [v[:, p] for p in parts], top)
        less = jnp.exp2(top - new)
        sum0, sum1 = sum0 * less, sum1 * less
        for p in parts:
            e = jnp.exp2(v[:, p] - new)
            sum0 = sum0 + e
            sum1 = sum1 + e * weight[:, p]
        return new, sum0, sum1

    zero = jnp.zeros((columns, 128), f32)
    top, sum0, sum1 = lax.fori_loop(0, tiles, column_step, (jnp.full((columns, 128), -1e30, f32), zero, zero))
    z = z_ref[0]
    h0, h1, f0, f1 = (z[emb + k : emb + k + 1] for k in range(4))
    offset = (-SCALE * f0 - math.log2(shelters), -SCALE * (h1 + f0 - h0) - math.log2(shelters))
    top, sum0, sum1 = top.T, sum0.T, sum1.T
    high = jnp.max(top, axis=0, keepdims=True)
    less = jnp.exp2(top - high)
    column_ref[0:1, :] = high + jnp.log2(jnp.sum(sum0 * less, axis=0, keepdims=True)) + offset[0]
    column_ref[1:2, :] = high + jnp.log2(jnp.sum(sum1 * less, axis=0, keepdims=True)) + offset[1]

    @pl.when(jnp.logical_not(near))
    def _():
        own = side_ref[left]
        for s in range(2):

            def exact(t, carry):
                at = pl.ds(pl.multiple_of(t * tile, tile), tile)

                def block(b, state):
                    side_ref[0] = y_side(z_ref[b], emb)
                    v = score(side_ref[0], other_ref[:, at])
                    if s:
                        v = v + wide(across(gap_of(z_ref[b], emb)), tile)
                    new = jnp.maximum(state[0], jnp.max(v, axis=0, keepdims=True))
                    return new, state[1] * jnp.exp2(state[0] - new) + jnp.sum(jnp.exp2(v - new), axis=0, keepdims=True)

                high, total = lax.fori_loop(0, blocks, block, (jnp.full((1, tile), -1e30, f32), jnp.zeros((1, tile), f32)))
                lse = high + jnp.log2(total)
                lse_ref[s : s + 1, at] = lse
                anchor_ref[s : s + 1, at] = (-EPSILON * math.log(shelters)) - (EPSILON * math.log(2.0)) * lse
                return carry

            lax.fori_loop(0, tiles, exact, 0)

            def column(t, state):
                at = pl.ds(pl.multiple_of(t * tile, tile), tile)
                v = score(own, other_ref[:, at]) - lse_ref[s : s + 1, at]
                new, total = state
                for k in range(tile // 128):
                    new = jnp.maximum(new, v[:, k * 128 : (k + 1) * 128])
                total = total * jnp.exp2(state[0] - new)
                for k in range(tile // 128):
                    total = total + jnp.exp2(v[:, k * 128 : (k + 1) * 128] - new)
                return new, total

            high, total = lax.fori_loop(0, tiles, column, (jnp.full((columns, 128), -1e30, f32), zero))
            high, total = high.T, total.T
            most = jnp.max(high, axis=0, keepdims=True)
            total = jnp.sum(total * jnp.exp2(high - most), axis=0, keepdims=True)
            column_ref[s : s + 1, :] = most + jnp.log2(total) + offset[s]


def on_device(anchor_embed, shelter_embed, hazard, shelter_pot):
    emb, rows = anchor_embed.shape
    columns = shelter_embed.shape[1]
    anchors = rows * lax.axis_size("orig")
    groups = lax.axis_size("shel")
    shelters = columns * groups
    tile = math.gcd(rows, 1024)
    f32 = jnp.float32
    vmem = pl.BlockSpec(memory_space=pltpu.VMEM)
    hbm = pl.BlockSpec(memory_space=pl.ANY)

    def scratch(blocks):
        return [
            pltpu.VMEM((emb, rows), f32),
            pltpu.SemaphoreType.DMA((rows // tile,)),
            pltpu.VMEM((blocks, columns, DEPTH), jnp.bfloat16),
            pltpu.VMEM((blocks, columns, 128), f32),
        ]

    def cost(blocks):
        return pl.CostEstimate(flops=2 * rows * columns * blocks * DEPTH, bytes_accessed=4 * rows * emb, transcendentals=rows * columns * blocks)

    def part(some):
        return pl.pallas_call(
            functools.partial(part_kernel, emb, tile),
            out_shape=jax.ShapeDtypeStruct((8, rows), f32),
            in_specs=[hbm, vmem],
            out_specs=vmem,
            scratch_shapes=scratch(some.shape[0]),
            compiler_params=pltpu.CompilerParams(vmem_limit_bytes=32 * 2**20),
            cost_estimate=cost(some.shape[0]),
        )(anchor_embed, some)

    every = jnp.concatenate([shelter_embed, hazard, shelter_pot], axis=0)[None]
    stats, known = [], []
    if groups & (groups - 1) == 0:
        far = 1
        while far < groups:
            got = lax.ppermute(every, "shel", [(k, k ^ far) for k in range(groups)])
            if far == 2:
                stats.append(part(every))
                known.append(far)
            elif far > 2:
                stats.append(part(every[far // 2 :]))
                known.append(far // 2)
            every = jnp.concatenate([every, got], axis=0)
            far *= 2
    else:
        other = [lax.ppermute(every, "shel", [(k, (k + d) % groups) for k in range(groups)]) for d in range(1, groups)]
        every = jnp.concatenate([every, *other])
    left = groups - sum(known)

    anchor_pot, column = pl.pallas_call(
        functools.partial(last_kernel, emb, tile, shelters, tuple(known)),
        out_shape=(jax.ShapeDtypeStruct((2, rows), f32), jax.ShapeDtypeStruct((2, columns), f32)),
        in_specs=[hbm] + [vmem] * (1 + len(stats)),
        out_specs=(vmem, vmem),
        scratch_shapes=[*scratch(left + 1), pltpu.VMEM((DEPTH, rows), jnp.bfloat16), pltpu.VMEM((2, rows), f32)],
        compiler_params=pltpu.CompilerParams(vmem_limit_bytes=48 * 2**20),
        cost_estimate=cost(left + 1),
    )(anchor_embed, every, *stats)

    halves = lax.axis_size("orig")
    parts = [column]
    for d in range(1, halves):
        parts.append(lax.ppermute(column, "orig", [(k, (k + d) % halves) for k in range(halves)]))
    high = functools.reduce(jnp.maximum, parts)
    total = sum(jnp.exp2(part - high) for part in parts)
    new_shelter_pot = -EPSILON * math.log(anchors) - (EPSILON * math.log(2.0)) * (high + jnp.log2(total))
    return anchor_pot, new_shelter_pot


def solution(mesh):
    placed = (
        P(None, ("region", "orig")),
        P(None, ("region", "shel")),
        P(None, ("region", "shel")),
        P(None, ("region", "shel")),
    )
    return jax.shard_map(
        on_device,
        mesh=mesh,
        in_specs=placed,
        out_specs=(P(None, ("region", "orig")), P(None, ("region", "shel"))),
        check_vma=False,
    )
```

time: 197 us -> 54.1 us (0.27)
  waiting for transfers between devices: 83.7 us -> 2.91 us
  other arithmetic: 50.2 us -> 1.38 us
  matrix products: 39.5 us -> 0 us
  Pallas kernels: 0 us -> 39.4 us
  between operations: 14.2 us -> 0.71 us
  starting transfers between devices: 0.26 us -> 7.8 us
  blocking collectives: 4.93 us -> 0 us
    all_gather x2 -> x0, waiting for transfers between devices: 83.2 us -> none  [merged(): everything = jax.tree.map(lambda part: lax.all_gather(part, axis), array)]
    dot_general x8 -> x0, matrix products: 39.5 us -> none  [tile_cost(): jnp.dot(xblock.T, shelter_embed, precision=lax.Precision.HIGHEST, preferr...]
    pallas_call x0 -> x3, Pallas kernels: none -> 39.4 us  [the longest x1 21.5 us: on_device(): pl.pallas_call(functools.partial(last_kernel, emb, tile, shelters, tuple(...]
    reduce_sum x17 -> x0, other arithmetic: 28.2 us -> none  [the longest x4 10.4 us: row_step(): total = jnp.sum(jnp.exp(score - top[:, :, None]), axis=2)]
    reduce_max x8 -> x0, other arithmetic: 12.8 us -> none  [the longest x4 8.07 us: col_step(): newtop = jnp.maximum(top, jnp.max(score, axis=1))]
    add x11 -> x0, other arithmetic: 8.43 us -> none  [the longest x7 8.37 us: joined(): first[1] * jnp.exp(first[0] - upper)]
    ppermute x0 -> x4, starting transfers between devices: none -> 7.8 us  [the longest x3 7.73 us: on_device(): got = lax.ppermute(every, 'shel', [(k, k ^ far) for k in range(groups)])]
    ppermute x0 -> x4, waiting for transfers between devices: none -> 2.91 us  [the longest x3 1.76 us: on_device(): got = lax.ppermute(every, 'shel', [(k, k ^ far) for k in range(groups)])]
  transfers between devices with their start and end apart: 2 -> 4, of which waited for: 2 -> 2; matrix products, arithmetic and copies ran while one was open for 0% -> 0% of each run, Pallas kernels for 0% -> 33%
where the time goes in v1:
time: 54.1 us; the launch traced here: 53.8 us
  Pallas kernels  39.4 us (73%)
  starting transfers between devices  7.8 us (14%)
  waiting for transfers between devices  2.91 us (5%)
  local copies, waits for them, and re-layouts  1.6 us (3%)
  other arithmetic  1.38 us (3%)
  between operations  0.71 us (1%)
    pallas_call x1, Pallas kernels, on_device(): pl.pallas_call(functools.partial(last_kernel, emb, tile, shelters, tuple(...  21.5 us
    pallas_call x2, Pallas kernels, part(): pl.pallas_call(functools.partial(part_kernel, emb, tile), out_shape=jax.S...  17.9 us
    ppermute x3, starting transfers between devices, on_device(): got = lax.ppermute(every, 'shel', [(k, k ^ far) for k in range(groups)])  7.73 us
    ppermute x3, waiting for transfers between devices, on_device(): got = lax.ppermute(every, 'shel', [(k, k ^ far) for k in range(groups)])  1.76 us
    unnamed x4, local copies, waits for them, and re-layouts  1.6 us
    ppermute x1, waiting for transfers between devices, on_device(): lax.ppermute(column, 'orig', [(k, (k + d) % halves) for k in range(halves)])  1.15 us
  transfers between devices with their start and end apart: 4, of which 2 were waited for; matrix products, arithmetic and copies ran while one was open for 0% of the time, Pallas kernels for 33%

profile of v1, /device:TPU:0, one launch (start us, length us, event | category | flops | bytes accessed | tf_op | source)
XLA Modules:
  0.0 53.8 jit_solution(13126827227498463125)
XLA Ops:
  0.6 0.8 %maximum_bitcast_fusion = f32[1,36,128]{2,1,0:T(8,128)S(1)} fusion(f32[2,128]{1,0:T(2,128)} %param.7, f32[2,128]{1,0:T(2,128)} %param.6, f32[32,128]{1,0:T(8,128)} %param.5), kind=kLoop, calls=%fused_computation.3 | loop fusion | flops 9216 | bytes 36864 | tf_op jit(solution)/shard_map/broadcast_in_dim | solution.py:277
  1.4 3.0 %collective-permute-start = (f32[1,36,128]{2,1,0:T(8,128)S(1)}, f32[1,36,128]{2,1,0:T(8,128)S(1)}, u32[]{:S(2)}, u32[]{:S(2)}) collective-permute-start(f32[1,36,128]{2,1,0:T(8,128)S(1)} %maximum_bitcast_fusion), channel_id=1, source_target_pairs={{0,1},{1,0},{2,3},{3,2},{4,5},{5,4},{6,7},{7,6},{8,9},{9,8},{10,11... | collective-permute-start | bytes 55304 | tf_op jit(solution)/shard_map/ppermute | solution.py:282
  4.4 1.8 %collective-permute-done = f32[1,36,128]{2,1,0:T(8,128)S(1)} collective-permute-done((f32[1,36,128]{2,1,0:T(8,128)S(1)}, f32[1,36,128]{2,1,0:T(8,128)S(1)}, u32[]{:S(2)}, u32[]{:S(2)}) %collective-permute-start) | collective-permute-done | bytes 18464 | tf_op jit(solution)/shard_map/ppermute | solution.py:282
  6.2 2.1 %collective-permute-start.1 = (f32[2,36,128]{2,1,0:T(8,128)S(1)}, f32[2,36,128]{2,1,0:T(8,128)S(1)}, u32[]{:S(2)}, u32[]{:S(2)}) collective-permute-start(f32[2,36,128]{2,1,0:T(8,128)S(1)} %pad_maximum_fusion.2.z_ref), channel_id=1, source_target_pairs={{0,2},{1,3},{2,0},{3,1},{4,6},{5,7},{6,4},{7,5},{8,10},{9,11},{10,... | collective-permute-start | bytes 110600 | tf_op jit(solution)/shard_map/ppermute | solution.py:282
  8.2 0.0 copy-start
  8.2 1.6 %copy-done = f32[32,16384]{1,0:T(8,128)S(1)} copy-done((f32[32,16384]{1,0:T(8,128)S(1)}, f32[32,16384]{1,0:T(8,128)}, u32[]{:S(2)}) %copy-start) | copy-done | bytes 2097176
  9.8 8.9 %shard_map.59.refs_0_ = f32[8,16384]{1,0:T(8,128)S(1)} custom-call(f32[32,16384]{1,0:T(8,128)S(1)} %copy-done, f32[2,36,128]{2,1,0:T(8,128)S(1)} %pad_maximum_fusion.2.z_ref), custom_call_target="tpu_custom_call" | custom-call | flops 2147483648 | bytes 2097152 | tf_op jit(solution)/shard_map/pallas_call | solution.py:267
  18.8 0.0 collective-permute-done.1.z_ref
  18.8 0.0 copy-start.1
  18.8 2.7 %collective-permute-start.2 = (f32[4,36,128]{2,1,0:T(8,128)S(1)}, f32[4,36,128]{2,1,0:T(8,128)S(1)}, u32[]{:S(2)}, u32[]{:S(2)}) collective-permute-start(f32[4,36,128]{2,1,0:T(8,128)S(1)} %pad_maximum_fusion.1), channel_id=1, source_target_pairs={{0,4},{1,5},{2,6},{3,7},{4,0},{5,1},{6,2},{7,3},{8,12},{9,13},{10,... | collective-permute-start | bytes 221192 | tf_op jit(solution)/shard_map/ppermute | solution.py:282
  21.5 8.9 %shard_map.60.refs_1_ = f32[8,16384]{1,0:T(8,128)S(1)} custom-call(f32[32,16384]{1,0:T(8,128)S(1)} %copy-done, f32[2,36,128]{2,1,0:T(8,128)S(1)} %collective-permute-done.1.z_ref), custom_call_target="tpu_custom_call" | custom-call | flops 2147483648 | bytes 2097152 | tf_op jit(solution)/shard_map/pallas_call | solution.py:267
  30.4 0.0 collective-permute-done.2
  30.4 0.0 copy-done.1
  30.4 21.5 %shard_map.61 = (f32[2,16384]{1,0:T(2,128)}, f32[2,128]{1,0:T(2,128)S(1)}) custom-call(f32[32,16384]{1,0:T(8,128)S(1)} %copy-done.1, f32[8,36,128]{2,1,0:T(8,128)S(1)} %pad_maximum_fusion.z_ref, f32[8,16384]{1,0:T(8,128)S(1)} %shard_map.59.refs_0_, f32[8,16384]{1,0:T(8,128)S(1)} %shard_map.60.refs_1_), custom_call_target="tpu_custom_call" | custom-call | flops 5368709120 | bytes 2097152 | tf_op jit(solution)/shard_map/pallas_call | solution.py:296
  52.0 0.1 collective-permute-start.3
  52.1 1.1 %collective-permute-done.3 = f32[2,128]{1,0:T(2,128)S(1)} collective-permute-done((f32[2,128]{1,0:T(2,128)S(1)}, f32[2,128]{1,0:T(2,128)S(1)}, u32[]{:S(2)}, u32[]{:S(2)}) %collective-permute-start.3) | collective-permute-done | bytes 1056 | tf_op jit(solution)/shard_map/ppermute | solution.py:309
  53.2 0.6 %multiply_subtract_fusion = f32[2,128]{1,0:T(2,128)} fusion(f32[2,128]{1,0:T(2,128)S(1)} %collective-permute-done.3, f32[2,128]{1,0:T(2,128)S(1)} %get-tuple-element.5), kind=kLoop, calls=%fused_computation.4 | loop fusion | flops 2560 | bytes 3072 | tf_op jit(solution)/shard_map/sub | solution.py:312
  (3 shorter events, 0.0 us)
Async XLA Ops:
  1.4 4.8 %collective-permute-start = (f32[1,36,128]{2,1,0:T(8,128)S(1)}, f32[1,36,128]{2,1,0:T(8,128)S(1)}, u32[]{:S(2)}, u32[]{:S(2)}) collective-permute-start(f32[1,36,128]{2,1,0:T(8,128)S(1)} %maximum_bitcast_fusion), channel_id=1, source_target_pairs={{0,1},{1,0},{2,3},{3,2},{4,5},{5,4},{6,7},{7,6},{8,9},{9,8},{10,11... | collective-permute-start | bytes 55304 | tf_op jit(solution)/shard_map/ppermute | solution.py:282
  6.2 12.6 %collective-permute-start.1 = (f32[2,36,128]{2,1,0:T(8,128)S(1)}, f32[2,36,128]{2,1,0:T(8,128)S(1)}, u32[]{:S(2)}, u32[]{:S(2)}) collective-permute-start(f32[2,36,128]{2,1,0:T(8,128)S(1)} %pad_maximum_fusion.2.z_ref), channel_id=1, source_target_pairs={{0,2},{1,3},{2,0},{3,1},{4,6},{5,7},{6,4},{7,5},{8,10},{9,11},{10,... | collective-permute-start | bytes 110600 | tf_op jit(solution)/shard_map/ppermute | solution.py:282
  8.2 1.6 %copy-start = (f32[32,16384]{1,0:T(8,128)S(1)}, f32[32,16384]{1,0:T(8,128)}, u32[]{:S(2)}) copy-start(f32[32,16384]{1,0:T(8,128)} %x_hbm.5) | copy-start | bytes 6291460
  18.8 11.6 %copy-start.1 = (f32[32,16384]{1,0:T(8,128)S(1)}, f32[32,16384]{1,0:T(8,128)}, u32[]{:S(2)}) copy-start(f32[32,16384]{1,0:T(8,128)} %x_hbm.5) | copy-start | bytes 6291460
  18.8 11.6 %collective-permute-start.2 = (f32[4,36,128]{2,1,0:T(8,128)S(1)}, f32[4,36,128]{2,1,0:T(8,128)S(1)}, u32[]{:S(2)}, u32[]{:S(2)}) collective-permute-start(f32[4,36,128]{2,1,0:T(8,128)S(1)} %pad_maximum_fusion.1), channel_id=1, source_target_pairs={{0,4},{1,5},{2,6},{3,7},{4,0},{5,1},{6,2},{7,3},{8,12},{9,13},{10,... | collective-permute-start | bytes 221192 | tf_op jit(solution)/shard_map/ppermute | solution.py:282
  52.0 1.2 %collective-permute-start.3 = (f32[2,128]{1,0:T(2,128)S(1)}, f32[2,128]{1,0:T(2,128)S(1)}, u32[]{:S(2)}, u32[]{:S(2)}) collective-permute-start(f32[2,128]{1,0:T(2,128)S(1)} %get-tuple-element.5), channel_id=1, source_target_pairs={{0,8},{8,0},{1,9},{9,1},{2,10},{10,2},{3,11},{11,3},{4,12},{12,4},... | collective-permute-start | bytes 3080 | tf_op jit(solution)/shard_map/ppermute | solution.py:309

commit v2 on v0

v2 whole, which is shorter than its diff:
```python
import functools
import math

import jax
import jax.numpy as jnp
from jax import lax
from jax.experimental import pallas as pl
from jax.experimental.pallas import tpu as pltpu
from jax.sharding import PartitionSpec as P

EPSILON = 0.25
SCALE = math.log2(math.e) / EPSILON
SPREAD = 36.0
DEPTH = 256


def three(v):
    a = v.astype(jnp.bfloat16).astype(jnp.float32)
    rest = v - a
    b = rest.astype(jnp.bfloat16).astype(jnp.float32)
    return a, b, (rest - b).astype(jnp.bfloat16).astype(jnp.float32)


def rows_of(values, count):
    width = next(v.shape[1] for v in values if not isinstance(v, float))
    index = lax.broadcasted_iota(jnp.int32, (count, width), 0)
    out = jnp.zeros((count, width), jnp.float32)
    for k, v in enumerate(values):
        out = jnp.where(index == k, v, out)
    return out


def x_side(x):
    emb = x.shape[0]
    x0, x1, x2 = three(x)
    norm = jnp.sum(x * x, axis=0, keepdims=True) * (-SCALE / emb)
    misc = rows_of((*three(norm), 1.0, 1.0, 1.0), DEPTH - 6 * emb)
    return jnp.concatenate([x0, x0, x1, x1, x0, x2, misc], axis=0).astype(jnp.bfloat16)


def gap_of(z, emb):
    h0, h1, f0, f1 = (z[emb + k : emb + k + 1] for k in range(4))
    return SCALE * ((f1 - h1) - (f0 - h0))


def y_side(z, emb):
    y = z[:emb]
    y0, y1, y2 = three(y * (2.0 * SCALE / emb))
    bias = SCALE * (z[emb + 2 : emb + 3] - z[emb : emb + 1]) - jnp.sum(y * y, axis=0, keepdims=True) * (SCALE / emb)
    misc = rows_of((1.0, 1.0, 1.0, *three(bias)), DEPTH - 6 * emb)
    side = jnp.concatenate([y0, y1, y0, y1, y2, y0, misc], axis=0)
    return side.T.astype(jnp.bfloat16)


def across(row):
    return jnp.broadcast_to(row, (128, row.shape[1])).T


def wide(block, width):
    return jnp.concatenate([block] * (width // 128), axis=1)


def score(side, other):
    return lax.dot_general(side, other, (((1,), (0,)), ((), ())), preferred_element_type=jnp.float32)


def row_sums(side, ratio, other):
    width = other.shape[1]
    count = side.shape[0]
    chunk = math.gcd(count, 128)
    v = score(side, other)
    state = None
    for c in range(0, count, chunk):
        part = v[c : c + chunk].reshape(chunk // 8, 8, width)
        r = wide(ratio[c : c + chunk], width).reshape(part.shape)
        new = jnp.max(part, axis=0)
        if state is not None:
            new = jnp.maximum(state[0], new)
        e = jnp.exp2(part - new)
        add0, add1 = jnp.sum(e, axis=0), jnp.sum(e * r, axis=0)
        if state is not None:
            less = jnp.exp2(state[0] - new)
            add0, add1 = state[1] * less + add0, state[2] * less + add1
        state = new, add0, add1
    return state


def merged(first, second):
    if first is None:
        return second
    high = jnp.maximum(first[0], second[0])
    one, two = jnp.exp2(first[0] - high), jnp.exp2(second[0] - high)
    return (high, *(a * one + b * two for a, b in zip(first[1:], second[1:])))


def one_row(state):
    top, sum0, sum1 = state
    high = jnp.max(top, axis=0, keepdims=True)
    less = jnp.exp2(top - high)
    return high, jnp.sum(sum0 * less, axis=0, keepdims=True), jnp.sum(sum1 * less, axis=0, keepdims=True)


def prepare(z, emb, side_ref, ratio_ref, slot):
    columns = z.shape[1]
    at = pl.ds(slot * columns, columns)
    side_ref[at, :] = y_side(z, emb)
    ratio_ref[at, :] = across(jnp.exp2(jnp.clip(gap_of(z, emb), -SPREAD, SPREAD)))


def all_rows(side_ref, ratio_ref, other):
    count = side_ref.shape[0]
    if count <= 512:
        return row_sums(side_ref[...], ratio_ref[...], other)

    def step(k, state):
        at = pl.ds(pl.multiple_of(k * 512, 512), 512)
        return merged(state, row_sums(side_ref[at, :], ratio_ref[at, :], other))

    return lax.fori_loop(1, count // 512, step, row_sums(side_ref[:512], ratio_ref[:512], other))


def starting(pairs, half):
    return pl.multiple_of(lax.rem(lax.axis_index("shel"), pairs) * half, half)


def anchors_kernel(tile, x_hbm, other_ref, x_ref, sems):
    def fetch(t):
        at = pl.ds(pl.multiple_of(t * tile, tile), tile)
        return pltpu.make_async_copy(x_hbm.at[:, at], x_ref.at[:, at], sems.at[t])

    tiles = x_ref.shape[1] // tile

    def begin(t, carry):
        fetch(t).start()
        return carry

    def step(t, carry):
        fetch(t).wait()
        at = pl.ds(pl.multiple_of(t * tile, tile), tile)
        other_ref[:, at] = x_side(x_ref[:, at])
        return carry

    lax.fori_loop(0, tiles, begin, 0)
    lax.fori_loop(0, tiles, step, 0)


def part_kernel(emb, tile, pairs, other_ref, z_ref, stat_ref, side_ref, ratio_ref):
    half = stat_ref.shape[1]
    start = starting(pairs, half)
    for b in range(z_ref.shape[0]):
        prepare(z_ref[b], emb, side_ref, ratio_ref, b)

    def step(t, carry):
        for part in range(0, tile, 256):
            at = pl.multiple_of(t * tile + part, 256)
            other = other_ref[:, pl.ds(pl.multiple_of(start + at, 256), 256)]
            for k, v in enumerate(one_row(all_rows(side_ref, ratio_ref, other))):
                stat_ref[k : k + 1, pl.ds(at, 256)] = v
        return carry

    lax.fori_loop(0, half // tile, step, 0)


def spread_of(z_ref, emb):
    z = z_ref[...]
    h0, h1, f0, f1 = (z[:, emb + k, :] for k in range(4))
    return jnp.max(jnp.abs(SCALE * ((f1 - h1) - (f0 - h0))))


def rest_kernel(emb, tile, pairs, first, other_ref, z_ref, *refs):
    *stats, lse_ref, side_ref, ratio_ref = refs
    blocks, _, columns = z_ref.shape
    half = lse_ref.shape[1]
    start = starting(pairs, half)
    for b in range(first, blocks) if blocks <= 8 else ():
        prepare(z_ref[b], emb, side_ref, ratio_ref, b - first)
    if blocks > 8:

        def ready(b, carry):
            prepare(z_ref[b], emb, side_ref, ratio_ref, b - first)
            return carry

        lax.fori_loop(first, blocks, ready, 0)
    near = spread_of(z_ref, emb) <= SPREAD

    def step(t, carry):
        for part in range(0, tile, 256):
            at = pl.multiple_of(t * tile + part, 256)
            other = other_ref[:, pl.ds(pl.multiple_of(start + at, 256), 256)]
            at = pl.ds(at, 256)
            state = one_row(all_rows(side_ref, ratio_ref, other))
            for ref in stats:
                state = merged(state, tuple(ref[k : k + 1, at] for k in range(3)))
            for s in range(2):
                lse_ref[s : s + 1, at] = state[0] + jnp.log2(state[1 + s])
        return carry

    lax.fori_loop(0, half // tile, step, 0)

    @pl.when(jnp.logical_not(near))
    def _():
        own = pl.ds(0, columns)
        for s in range(2):

            def exact(t, carry):
                at = pl.multiple_of(t * 256, 256)
                other = other_ref[:, pl.ds(pl.multiple_of(start + at, 256), 256)]

                def block(b, state):
                    side_ref[own, :] = y_side(z_ref[b], emb)
                    v = score(side_ref[own, :], other)
                    if s:
                        v = v + wide(across(gap_of(z_ref[b], emb)), 256)
                    high = jnp.max(v, axis=0, keepdims=True)
                    return merged(state, (high, jnp.sum(jnp.exp2(v - high), axis=0, keepdims=True)))

                none = (jnp.full((1, 256), -1e30, jnp.float32), jnp.zeros((1, 256), jnp.float32))
                high, total = lax.fori_loop(0, blocks, block, none)
                lse_ref[s : s + 1, pl.ds(at, 256)] = high + jnp.log2(total)
                return carry

            lax.fori_loop(0, half // 256, exact, 0)


def column_sums(side, other_ref, start, lse_ref, tile, state_refs):
    columns = side.shape[0]

    def step(t, carry):
        at = pl.multiple_of(t * tile, tile)
        lse = lse_ref[0:1, pl.ds(at, tile)]
        weight = jnp.exp2(jnp.clip(lse - lse_ref[1:2, pl.ds(at, tile)], -SPREAD, SPREAD))
        lse, weight = jnp.broadcast_to(lse, (8, tile)), jnp.broadcast_to(weight, (8, tile))
        v = score(side, other_ref[:, pl.ds(pl.multiple_of(start + at, tile), tile)])
        parts = [slice(k, k + 128) for k in range(0, tile, 128)]
        for g in range(0, columns, 8):
            rows = slice(g, g + 8)
            u = [v[rows, p] - lse[:, p] for p in parts]
            top, sum0, sum1 = (ref[rows, :] for ref in state_refs)
            new = functools.reduce(jnp.maximum, u, top)
            less = jnp.exp2(top - new)
            e = [jnp.exp2(w - new) for w in u]
            state_refs[0][rows, :] = new
            state_refs[1][rows, :] = functools.reduce(jnp.add, e, sum0 * less)
            state_refs[2][rows, :] = functools.reduce(jnp.add, [w * weight[:, p] for w, p in zip(e, parts)], sum1 * less)
        return carry

    lax.fori_loop(0, lse_ref.shape[1] // tile, step, 0)


def columns_kernel(emb, tile, pairs, other_ref, z_ref, lse_ref, top_ref, sum0_ref, sum1_ref, side_ref):
    half = lse_ref.shape[1]
    side_ref[...] = y_side(z_ref[0], emb)
    top_ref[...] = jnp.full(top_ref.shape, -1e30, jnp.float32)
    sum0_ref[...] = jnp.zeros(sum0_ref.shape, jnp.float32)
    sum1_ref[...] = jnp.zeros(sum1_ref.shape, jnp.float32)
    column_sums(side_ref[...], other_ref, starting(pairs, half), lse_ref, tile, (top_ref, sum0_ref, sum1_ref))


def finish_kernel(emb, tile, pairs, shelters, other_ref, z_ref, *refs):
    lse_refs, refs = refs[:pairs], refs[pairs:]
    *old, anchor_ref, column_ref, top_ref, sum0_ref, sum1_ref, side_ref = refs
    half = lse_refs[0].shape[1]
    mine = lax.rem(lax.axis_index("shel"), pairs)
    near = spread_of(z_ref, emb) <= SPREAD
    starts = [pl.multiple_of((mine ^ k) * half, half) for k in range(pairs)]
    side_ref[...] = y_side(z_ref[0], emb)
    states = (top_ref, sum0_ref, sum1_ref)
    for new, ref in zip(states, old):
        new[...] = ref[...]
    for start, lse_ref in list(zip(starts, lse_refs))[1:]:
        column_sums(side_ref[...], other_ref, start, lse_ref, tile, states)
    z = z_ref[0]
    h0, h1, f0, f1 = (z[emb + k : emb + k + 1] for k in range(4))
    offset = (-SCALE * f0 - math.log2(shelters), -SCALE * (h1 + f0 - h0) - math.log2(shelters))

    def one(top, *sums):
        top = top.T
        high = jnp.max(top, axis=0, keepdims=True)
        less = jnp.exp2(top - high)
        return [high + jnp.log2(jnp.sum(s.T * less, axis=0, keepdims=True)) for s in sums]

    for s, v in enumerate(one(*(ref[...] for ref in states))):
        column_ref[s : s + 1, :] = v + offset[s]
    for start, lse_ref in zip(starts, lse_refs):
        anchor_ref[:, pl.ds(start, half)] = (-EPSILON * math.log(shelters)) - (EPSILON * math.log(2.0)) * lse_ref[...]

    @pl.when(jnp.logical_not(near))
    def _():
        for s in range(2):
            top_ref[...] = jnp.full(top_ref.shape, -1e30, jnp.float32)
            sum0_ref[...] = jnp.zeros(sum0_ref.shape, jnp.float32)
            for start, lse_ref in zip(starts, lse_refs):

                def column(t, carry):
                    at = pl.multiple_of(t * 256, 256)
                    other = other_ref[:, pl.ds(pl.multiple_of(start + at, 256), 256)]
                    v = score(side_ref[...], other) - lse_ref[s : s + 1, pl.ds(at, 256)]
                    top = top_ref[...]
                    new = jnp.maximum(top, jnp.maximum(v[:, :128], v[:, 128:]))
                    sum0_ref[...] = sum0_ref[...] * jnp.exp2(top - new) + jnp.exp2(v[:, :128] - new) + jnp.exp2(v[:, 128:] - new)
                    top_ref[...] = new
                    return carry

                lax.fori_loop(0, half // 256, column, 0)
            column_ref[s : s + 1, :] = one(top_ref[...], sum0_ref[...])[0] + offset[s]


def swapped(value, far, groups):
    return lax.ppermute(value, "shel", [(k, k ^ far) for k in range(groups)])


def on_device(anchor_embed, shelter_embed, hazard, shelter_pot):
    emb, rows = anchor_embed.shape
    columns = shelter_embed.shape[1]
    anchors = rows * lax.axis_size("orig")
    groups = lax.axis_size("shel")
    shelters = columns * groups
    pairs = 2 if groups % 2 == 0 else 1
    half = rows // pairs
    f32, bf16 = jnp.float32, jnp.bfloat16
    vmem = pl.BlockSpec(memory_space=pltpu.VMEM)

    def call(kernel, outs, ins, scratch, work, first=vmem):
        return pl.pallas_call(
            kernel,
            out_shape=outs,
            in_specs=[first] + [vmem] * (len(ins) - 1),
            out_specs=jax.tree.map(lambda _: vmem, outs),
            scratch_shapes=scratch,
            compiler_params=pltpu.CompilerParams(vmem_limit_bytes=24 * 2**20),
            cost_estimate=pl.CostEstimate(flops=2 * DEPTH * work, bytes_accessed=DEPTH * rows, transcendentals=work),
        )(*ins)

    def sides(blocks):
        return [pltpu.VMEM((blocks * columns, DEPTH), bf16), pltpu.VMEM((blocks * columns, 128), f32)]

    shape = jax.ShapeDtypeStruct
    every = jnp.concatenate([shelter_embed, hazard, shelter_pot], axis=0)[None]
    tile = math.gcd(rows, 1024)
    other = call(
        functools.partial(anchors_kernel, tile),
        shape((DEPTH, rows), bf16),
        [anchor_embed],
        [pltpu.VMEM((emb, rows), f32), pltpu.SemaphoreType.DMA((rows // tile,))],
        64 * rows,
        pl.BlockSpec(memory_space=pltpu.HBM),
    )

    tile = math.gcd(half, 1024)

    def part(some):
        blocks = some.shape[0]
        return call(
            functools.partial(part_kernel, emb, tile, pairs),
            shape((8, half), f32),
            [other, some],
            sides(blocks),
            half * columns * blocks,
        )

    stats, done = [], 0
    if groups & (groups - 1) == 0:
        far = 1
        while far < groups:
            got = swapped(every, far, groups)
            if far > 1:
                stats.append(part(every[done:]))
                done = far
            every = jnp.concatenate([every, got], axis=0)
            far *= 2
    else:
        blocks = [lax.ppermute(every, "shel", [(k, (k + d) % groups) for k in range(groups)]) for d in range(1, groups)]
        every = jnp.concatenate([every, *blocks])
    lse = call(
        functools.partial(rest_kernel, emb, tile, pairs, done),
        shape((2, half), f32),
        [other, every, *stats],
        sides(groups - done),
        half * columns * (groups - done),
    )

    tile = math.gcd(half, 2048)
    state = [shape((columns, 128), f32)] * 3
    lses = [lse] + ([swapped(lse, 1, groups)] if pairs == 2 else [])
    sums = call(
        functools.partial(columns_kernel, emb, tile, pairs),
        state,
        [other, every, lse],
        [pltpu.VMEM((columns, DEPTH), bf16)],
        half * columns,
    )
    anchor_pot, column = call(
        functools.partial(finish_kernel, emb, tile, pairs, shelters),
        (shape((2, rows), f32), shape((2, columns), f32)),
        [other, every, *lses, *sums],
        [pltpu.VMEM(s.shape, f32) for s in state] + [pltpu.VMEM((columns, DEPTH), bf16)],
        half * columns,
    )

    halves = lax.axis_size("orig")
    parts = [column]
    for d in range(1, halves):
        parts.append(lax.ppermute(column, "orig", [(k, (k + d) % halves) for k in range(halves)]))
    high = functools.reduce(jnp.maximum, parts)
    total = sum(jnp.exp2(part - high) for part in parts)
    new_shelter_pot = -EPSILON * math.log(anchors) - (EPSILON * math.log(2.0)) * (high + jnp.log2(total))
    return anchor_pot, new_shelter_pot


def solution(mesh):
    placed = (
        P(None, ("region", "orig")),
        P(None, ("region", "shel")),
        P(None, ("region", "shel")),
        P(None, ("region", "shel")),
    )
    return jax.shard_map(
        on_device,
        mesh=mesh,
        in_specs=placed,
        out_specs=(P(None, ("region", "orig")), P(None, ("region", "shel"))),
        check_vma=False,
    )
```

time: 197 us -> 36.1 us (0.18)
  waiting for transfers between devices: 83.7 us -> 2.83 us
  other arithmetic: 50.2 us -> 1.38 us
  matrix products: 39.5 us -> 0 us
  Pallas kernels: 0 us -> 21.5 us
  between operations: 14.2 us -> 0.72 us
  starting transfers between devices: 0.26 us -> 7.87 us
  blocking collectives: 4.93 us -> 0 us
    all_gather x2 -> x0, waiting for transfers between devices: 83.2 us -> none  [merged(): everything = jax.tree.map(lambda part: lax.all_gather(part, axis), array)]
    dot_general x8 -> x0, matrix products: 39.5 us -> none  [tile_cost(): jnp.dot(xblock.T, shelter_embed, precision=lax.Precision.HIGHEST, preferr...]
    reduce_sum x17 -> x0, other arithmetic: 28.2 us -> none  [the longest x4 10.4 us: row_step(): total = jnp.sum(jnp.exp(score - top[:, :, None]), axis=2)]
    pallas_call x0 -> x6, Pallas kernels: none -> 21.5 us  [call(): pl.pallas_call(kernel, out_shape=outs, in_specs=[first] + [vmem] * (len(i...]
    reduce_max x8 -> x0, other arithmetic: 12.8 us -> none  [the longest x4 8.07 us: col_step(): newtop = jnp.maximum(top, jnp.max(score, axis=1))]
    add x11 -> x0, other arithmetic: 8.43 us -> none  [the longest x7 8.37 us: joined(): first[1] * jnp.exp(first[0] - upper)]
    ppermute x0 -> x5, starting transfers between devices: none -> 7.87 us  [the longest x4 7.87 us: swapped(): return lax.ppermute(value, 'shel', [(k, k ^ far) for k in range(groups)])]
    ppermute x0 -> x5, waiting for transfers between devices: none -> 2.83 us  [the longest x4 1.67 us: swapped(): return lax.ppermute(value, 'shel', [(k, k ^ far) for k in range(groups)])]
  transfers between devices with their start and end apart: 2 -> 5, of which waited for: 2 -> 2; matrix products, arithmetic and copies ran while one was open for 0% -> 0% of each run, Pallas kernels for 0% -> 34%
where the time goes in v2:
time: 36.1 us; the launch traced here: 35.9 us
  Pallas kernels  21.5 us (60%)
  starting transfers between devices  7.87 us (22%)
  waiting for transfers between devices  2.83 us (8%)
  local copies, waits for them, and re-layouts  1.59 us (4%)
  other arithmetic  1.38 us (4%)
  between operations  0.72 us (2%)
    pallas_call x6, Pallas kernels, call(): pl.pallas_call(kernel, out_shape=outs, in_specs=[first] + [vmem] * (len(i...  21.5 us
    ppermute x4, starting transfers between devices, swapped(): return lax.ppermute(value, 'shel', [(k, k ^ far) for k in range(groups)])  7.87 us
    ppermute x4, waiting for transfers between devices, swapped(): return lax.ppermute(value, 'shel', [(k, k ^ far) for k in range(groups)])  1.67 us
    unnamed x2, local copies, waits for them, and re-layouts  1.59 us
    ppermute x1, waiting for transfers between devices, on_device(): lax.ppermute(column, 'orig', [(k, (k + d) % halves) for k in range(halves)])  1.16 us
    broadcast_in_dim x1, other arithmetic, on_device(): every = jnp.concatenate([shelter_embed, hazard, shelter_pot], axis=0)[None]  0.76 us
  transfers between devices with their start and end apart: 5, of which 2 were waited for; matrix products, arithmetic and copies ran while one was open for 0% of the time, Pallas kernels for 34%

profile of v2, /device:TPU:0, one launch (start us, length us, event | category | flops | bytes accessed | tf_op | source)
XLA Modules:
  0.0 35.9 jit_solution(13982459795120202613)
XLA Ops:
  0.6 0.8 %maximum_bitcast_fusion = f32[1,36,128]{2,1,0:T(8,128)S(1)} fusion(f32[2,128]{1,0:T(2,128)} %param.7, f32[2,128]{1,0:T(2,128)} %param.6, f32[32,128]{1,0:T(8,128)} %param.5), kind=kLoop, calls=%fused_computation.3 | loop fusion | flops 9216 | bytes 36864 | tf_op jit(solution)/shard_map/broadcast_in_dim | solution.py:338
  1.4 3.0 %collective-permute-start = (f32[1,36,128]{2,1,0:T(8,128)S(1)}, f32[1,36,128]{2,1,0:T(8,128)S(1)}, u32[]{:S(2)}, u32[]{:S(2)}) collective-permute-start(f32[1,36,128]{2,1,0:T(8,128)S(1)} %maximum_bitcast_fusion), channel_id=1, source_target_pairs={{0,1},{1,0},{2,3},{3,2},{4,5},{5,4},{6,7},{7,6},{8,9},{9,8},{10,11... | collective-permute-start | bytes 55304 | tf_op jit(solution)/shard_map/ppermute | solution.py:309
  4.4 0.0 copy-start
  4.4 1.6 %copy-done = f32[32,16384]{1,0:T(8,128)S(1)} copy-done((f32[32,16384]{1,0:T(8,128)S(1)}, f32[32,16384]{1,0:T(8,128)}, u32[]{:S(2)}) %copy-start) | copy-done | bytes 2097176
  6.0 2.2 %shard_map.59.other_ref = bf16[256,16384]{1,0:T(8,128)(2,1)S(1)} custom-call(f32[32,16384]{1,0:T(8,128)S(1)} %copy-done), custom_call_target="tpu_custom_call" | custom-call | flops 536870912 | bytes 4194304 | tf_op jit(solution)/shard_map/pallas_call | solution.py:324
  8.1 0.0 collective-permute-done
  8.2 1.6 %collective-permute-start.1 = (f32[2,36,128]{2,1,0:T(8,128)S(1)}, f32[2,36,128]{2,1,0:T(8,128)S(1)}, u32[]{:S(2)}, u32[]{:S(2)}) collective-permute-start(f32[2,36,128]{2,1,0:T(8,128)S(1)} %pad_maximum_fusion.2.z_ref), channel_id=1, source_target_pairs={{0,2},{1,3},{2,0},{3,1},{4,6},{5,7},{6,4},{7,5},{8,10},{9,11},{10,... | collective-permute-start | bytes 110600 | tf_op jit(solution)/shard_map/ppermute | solution.py:309
  9.8 3.9 %shard_map.60.refs_0_ = f32[8,8192]{1,0:T(8,128)S(1)} custom-call(bf16[256,16384]{1,0:T(8,128)(2,1)S(1)} %shard_map.59.other_ref, f32[2,36,128]{2,1,0:T(8,128)S(1)} %pad_maximum_fusion.2.z_ref), custom_call_target="tpu_custom_call" | custom-call | flops 1073741824 | bytes 4194304 | tf_op jit(solution)/shard_map/pallas_call | solution.py:324
  13.7 0.0 collective-permute-done.1.z_ref
  13.7 2.7 %collective-permute-start.2 = (f32[4,36,128]{2,1,0:T(8,128)S(1)}, f32[4,36,128]{2,1,0:T(8,128)S(1)}, u32[]{:S(2)}, u32[]{:S(2)}) collective-permute-start(f32[4,36,128]{2,1,0:T(8,128)S(1)} %pad_maximum_fusion.1), channel_id=1, source_target_pairs={{0,4},{1,5},{2,6},{3,7},{4,0},{5,1},{6,2},{7,3},{8,12},{9,13},{10,... | collective-permute-start | bytes 221192 | tf_op jit(solution)/shard_map/ppermute | solution.py:309
  16.4 3.9 %shard_map.61.refs_1_ = f32[8,8192]{1,0:T(8,128)S(1)} custom-call(bf16[256,16384]{1,0:T(8,128)(2,1)S(1)} %shard_map.59.other_ref, f32[2,36,128]{2,1,0:T(8,128)S(1)} %collective-permute-done.1.z_ref), custom_call_target="tpu_custom_call" | custom-call | flops 1073741824 | bytes 4194304 | tf_op jit(solution)/shard_map/pallas_call | solution.py:324
  20.3 0.0 collective-permute-done.2
  20.4 6.5 %shard_map.62.lse_ref.refs_0_ = f32[2,8192]{1,0:T(2,128)S(1)} custom-call(bf16[256,16384]{1,0:T(8,128)(2,1)S(1)} %shard_map.59.other_ref, f32[8,36,128]{2,1,0:T(8,128)S(1)} %pad_maximum_fusion.z_ref, f32[8,8192]{1,0:T(8,128)S(1)} %shard_map.60.refs_0_, f32[8,8192]{1,0:T(8,128)S(1)} %shard_map.61.refs_1_), custom_call_target="tpu_custom_call" | custom-call | flops 2147483648 | bytes 4194304 | tf_op jit(solution)/shard_map/pallas_call | solution.py:324
  26.9 0.6 %collective-permute-start.3 = (f32[2,8192]{1,0:T(2,128)S(1)}, f32[2,8192]{1,0:T(2,128)S(1)}, u32[]{:S(2)}, u32[]{:S(2)}) collective-permute-start(f32[2,8192]{1,0:T(2,128)S(1)} %shard_map.62.lse_ref.refs_0_), channel_id=1, source_target_pairs={{0,1},{1,0},{2,3},{3,2},{4,5},{5,4},{6,7},{7,6},{8,9},{9,8},{10,11... | collective-permute-start | bytes 196616 | tf_op jit(solution)/shard_map/ppermute | solution.py:309
  27.4 2.1 %shard_map.63 = (f32[128,128]{1,0:T(8,128)S(1)}, f32[128,128]{1,0:T(8,128)S(1)}, f32[128,128]{1,0:T(8,128)S(1)}) custom-call(bf16[256,16384]{1,0:T(8,128)(2,1)S(1)} %shard_map.59.other_ref, f32[8,36,128]{2,1,0:T(8,128)S(1)} %pad_maximum_fusion.z_ref, f32[2,8192]{1,0:T(2,128)S(1)} %shard_map.62.lse_ref.refs_0_), custom_call_target="tpu_custom_call" | custom-call | flops 536870912 | bytes 4194304 | tf_op jit(solution)/shard_map/pallas_call | solution.py:324
  29.5 1.7 %collective-permute-done.3.refs_1_ = f32[2,8192]{1,0:T(2,128)S(1)} collective-permute-done((f32[2,8192]{1,0:T(2,128)S(1)}, f32[2,8192]{1,0:T(2,128)S(1)}, u32[]{:S(2)}, u32[]{:S(2)}) %collective-permute-start.3) | collective-permute-done | bytes 65568 | tf_op jit(solution)/shard_map/ppermute | solution.py:309
  31.2 2.9 %shard_map.64 = (f32[2,16384]{1,0:T(2,128)}, f32[2,128]{1,0:T(2,128)S(1)}) custom-call(bf16[256,16384]{1,0:T(8,128)(2,1)S(1)} %shard_map.59.other_ref, f32[8,36,128]{2,1,0:T(8,128)S(1)} %pad_maximum_fusion.z_ref, f32[2,8192]{1,0:T(2,128)S(1)} %shard_map.62.lse_ref.refs_0_, f32[2,8192]{1,0:T(2,128)S(1)} %collective-permute-done.3.refs_1_, ...), custom_call_target="tpu_custom_call" | custom-call | flops 536870912 | bytes 4194304 | tf_op jit(solution)/shard_map/pallas_call | solution.py:324
  34.1 0.0 collective-permute-start.4
  34.1 1.2 %collective-permute-done.4 = f32[2,128]{1,0:T(2,128)S(1)} collective-permute-done((f32[2,128]{1,0:T(2,128)S(1)}, f32[2,128]{1,0:T(2,128)S(1)}, u32[]{:S(2)}, u32[]{:S(2)}) %collective-permute-start.4) | collective-permute-done | bytes 1056 | tf_op jit(solution)/shard_map/ppermute | solution.py:403
  35.3 0.6 %multiply_subtract_fusion = f32[2,128]{1,0:T(2,128)} fusion(f32[2,128]{1,0:T(2,128)S(1)} %collective-permute-done.4, f32[2,128]{1,0:T(2,128)S(1)} %get-tuple-element.11), kind=kLoop, calls=%fused_computation.4 | loop fusion | flops 2560 | bytes 3072 | tf_op jit(solution)/shard_map/sub | solution.py:406
  (3 shorter events, 0.0 us)
Async XLA Ops:
  1.4 6.8 %collective-permute-start = (f32[1,36,128]{2,1,0:T(8,128)S(1)}, f32[1,36,128]{2,1,0:T(8,128)S(1)}, u32[]{:S(2)}, u32[]{:S(2)}) collective-permute-start(f32[1,36,128]{2,1,0:T(8,128)S(1)} %maximum_bitcast_fusion), channel_id=1, source_target_pairs={{0,1},{1,0},{2,3},{3,2},{4,5},{5,4},{6,7},{7,6},{8,9},{9,8},{10,11... | collective-permute-start | bytes 55304 | tf_op jit(solution)/shard_map/ppermute | solution.py:309
  4.4 1.6 %copy-start = (f32[32,16384]{1,0:T(8,128)S(1)}, f32[32,16384]{1,0:T(8,128)}, u32[]{:S(2)}) copy-start(f32[32,16384]{1,0:T(8,128)} %x_hbm.1) | copy-start | bytes 6291460
  8.2 5.6 %collective-permute-start.1 = (f32[2,36,128]{2,1,0:T(8,128)S(1)}, f32[2,36,128]{2,1,0:T(8,128)S(1)}, u32[]{:S(2)}, u32[]{:S(2)}) collective-permute-start(f32[2,36,128]{2,1,0:T(8,128)S(1)} %pad_maximum_fusion.2.z_ref), channel_id=1, source_target_pairs={{0,2},{1,3},{2,0},{3,1},{4,6},{5,7},{6,4},{7,5},{8,10},{9,11},{10,... | collective-permute-start | bytes 110600 | tf_op jit(solution)/shard_map/ppermute | solution.py:309
  13.7 6.6 %collective-permute-start.2 = (f32[4,36,128]{2,1,0:T(8,128)S(1)}, f32[4,36,128]{2,1,0:T(8,128)S(1)}, u32[]{:S(2)}, u32[]{:S(2)}) collective-permute-start(f32[4,36,128]{2,1,0:T(8,128)S(1)} %pad_maximum_fusion.1), channel_id=1, source_target_pairs={{0,4},{1,5},{2,6},{3,7},{4,0},{5,1},{6,2},{7,3},{8,12},{9,13},{10,... | collective-permute-start | bytes 221192 | tf_op jit(solution)/shard_map/ppermute | solution.py:309
  26.9 4.3 %collective-permute-start.3 = (f32[2,8192]{1,0:T(2,128)S(1)}, f32[2,8192]{1,0:T(2,128)S(1)}, u32[]{:S(2)}, u32[]{:S(2)}) collective-permute-start(f32[2,8192]{1,0:T(2,128)S(1)} %shard_map.62.lse_ref.refs_0_), channel_id=1, source_target_pairs={{0,1},{1,0},{2,3},{3,2},{4,5},{5,4},{6,7},{7,6},{8,9},{9,8},{10,11... | collective-permute-start | bytes 196616 | tf_op jit(solution)/shard_map/ppermute | solution.py:309
  34.1 1.2 %collective-permute-start.4 = (f32[2,128]{1,0:T(2,128)S(1)}, f32[2,128]{1,0:T(2,128)S(1)}, u32[]{:S(2)}, u32[]{:S(2)}) collective-permute-start(f32[2,128]{1,0:T(2,128)S(1)} %get-tuple-element.11), channel_id=1, source_target_pairs={{0,8},{8,0},{1,9},{9,1},{2,10},{10,2},{3,11},{11,3},{4,12},{12,4},... | collective-permute-start | bytes 3080 | tf_op jit(solution)/shard_map/ppermute | solution.py:403

commit v3 on v2

--- a/solution.py
+++ b/solution.py
@@ -11,6 +11,7 @@
 EPSILON = 0.25
 SCALE = math.log2(math.e) / EPSILON
 SPREAD = 36.0
+PIECE = 512
 DEPTH = 256
 
 
@@ -119,29 +120,23 @@
     return lax.fori_loop(1, count // 512, step, row_sums(side_ref[:512], ratio_ref[:512], other))
 
 
+def anchors_at(other_ref, start, width):
+    first = start // 128
+    return jnp.concatenate([other_ref[first + k] for k in range(width // 128)], axis=1)
+
+
 def starting(pairs, half):
     return pl.multiple_of(lax.rem(lax.axis_index("shel"), pairs) * half, half)
 
 
-def anchors_kernel(tile, x_hbm, other_ref, x_ref, sems):
-    def fetch(t):
-        at = pl.ds(pl.multiple_of(t * tile, tile), tile)
-        return pltpu.make_async_copy(x_hbm.at[:, at], x_ref.at[:, at], sems.at[t])
-
-    tiles = x_ref.shape[1] // tile
-
-    def begin(t, carry):
-        fetch(t).start()
+def anchors_kernel(tile, x_ref, other_ref):
+    def step(t, carry):
+        side = x_side(x_ref[:, pl.ds(pl.multiple_of(t * tile, tile), tile)])
+        for k in range(tile // 128):
+            other_ref[t * (tile // 128) + k] = side[:, k * 128 : (k + 1) * 128]
         return carry
 
-    def step(t, carry):
-        fetch(t).wait()
-        at = pl.ds(pl.multiple_of(t * tile, tile), tile)
-        other_ref[:, at] = x_side(x_ref[:, at])
-        return carry
-
-    lax.fori_loop(0, tiles, begin, 0)
-    lax.fori_loop(0, tiles, step, 0)
+    lax.fori_loop(0, x_ref.shape[1] // tile, step, 0)
 
 
 def part_kernel(emb, tile, pairs, other_ref, z_ref, stat_ref, side_ref, ratio_ref):
@@ -151,10 +146,13 @@
         prepare(z_ref[b], emb, side_ref, ratio_ref, b)
 
     def step(t, carry):
+        found = []
         for part in range(0, tile, 256):
             at = pl.multiple_of(t * tile + part, 256)
-            other = other_ref[:, pl.ds(pl.multiple_of(start + at, 256), 256)]
-            for k, v in enumerate(one_row(all_rows(side_ref, ratio_ref, other))):
+            other = anchors_at(other_ref, start + at, 256)
+            found.append((at, one_row(all_rows(side_ref, ratio_ref, other))))
+        for at, state in found:
+            for k, v in enumerate(state):
                 stat_ref[k : k + 1, pl.ds(at, 256)] = v
         return carry
 
@@ -184,13 +182,16 @@
     near = spread_of(z_ref, emb) <= SPREAD
 
     def step(t, carry):
+        found = []
         for part in range(0, tile, 256):
             at = pl.multiple_of(t * tile + part, 256)
-            other = other_ref[:, pl.ds(pl.multiple_of(start + at, 256), 256)]
+            other = anchors_at(other_ref, start + at, 256)
             at = pl.ds(at, 256)
             state = one_row(all_rows(side_ref, ratio_ref, other))
             for ref in stats:
                 state = merged(state, tuple(ref[k : k + 1, at] for k in range(3)))
+            found.append((at, state))
+        for at, state in found:
             for s in range(2):
                 lse_ref[s : s + 1, at] = state[0] + jnp.log2(state[1 + s])
         return carry
@@ -204,7 +205,7 @@
 
             def exact(t, carry):
                 at = pl.multiple_of(t * 256, 256)
-                other = other_ref[:, pl.ds(pl.multiple_of(start + at, 256), 256)]
+                other = anchors_at(other_ref, start + at, 256)
 
                 def block(b, state):
                     side_ref[own, :] = y_side(z_ref[b], emb)
@@ -224,14 +225,13 @@
 
 def column_sums(side, other_ref, start, lse_ref, tile, state_refs):
     columns = side.shape[0]
-
-    def step(t, carry):
-        at = pl.multiple_of(t * tile, tile)
-        lse = lse_ref[0:1, pl.ds(at, tile)]
-        weight = jnp.exp2(jnp.clip(lse - lse_ref[1:2, pl.ds(at, tile)], -SPREAD, SPREAD))
-        lse, weight = jnp.broadcast_to(lse, (8, tile)), jnp.broadcast_to(weight, (8, tile))
-        v = score(side, other_ref[:, pl.ds(pl.multiple_of(start + at, tile), tile)])
-        parts = [slice(k, k + 128) for k in range(0, tile, 128)]
+    piece = math.gcd(tile, PIECE)
+
+    def some(at, v):
+        lse = lse_ref[0:1, pl.ds(at, piece)]
+        weight = jnp.exp2(jnp.clip(lse - lse_ref[1:2, pl.ds(at, piece)], -SPREAD, SPREAD))
+        lse, weight = jnp.broadcast_to(lse, (8, piece)), jnp.broadcast_to(weight, (8, piece))
+        parts = [slice(k, k + 128) for k in range(0, piece, 128)]
         for g in range(0, columns, 8):
             rows = slice(g, g + 8)
             u = [v[rows, p] - lse[:, p] for p in parts]
@@ -242,6 +242,12 @@
             state_refs[0][rows, :] = new
             state_refs[1][rows, :] = functools.reduce(jnp.add, e, sum0 * less)
             state_refs[2][rows, :] = functools.reduce(jnp.add, [w * weight[:, p] for w, p in zip(e, parts)], sum1 * less)
+
+    def step(t, carry):
+        ats = [pl.multiple_of(t * tile + k, piece) for k in range(0, tile, piece)]
+        scores = [score(side, anchors_at(other_ref, start + at, piece)) for at in ats]
+        for at, v in zip(ats, scores):
+            some(at, v)
         return carry
 
     lax.fori_loop(0, lse_ref.shape[1] // tile, step, 0)
@@ -293,7 +299,7 @@
 
                 def column(t, carry):
                     at = pl.multiple_of(t * 256, 256)
-                    other = other_ref[:, pl.ds(pl.multiple_of(start + at, 256), 256)]
+                    other = anchors_at(other_ref, start + at, 256)
                     v = score(side_ref[...], other) - lse_ref[s : s + 1, pl.ds(at, 256)]
                     top = top_ref[...]
                     new = jnp.maximum(top, jnp.maximum(v[:, :128], v[:, 128:]))
@@ -320,11 +326,11 @@
     f32, bf16 = jnp.float32, jnp.bfloat16
     vmem = pl.BlockSpec(memory_space=pltpu.VMEM)
 
-    def call(kernel, outs, ins, scratch, work, first=vmem):
+    def call(kernel, outs, ins, scratch, work):
         return pl.pallas_call(
             kernel,
             out_shape=outs,
-            in_specs=[first] + [vmem] * (len(ins) - 1),
+            in_specs=[vmem] * len(ins),
             out_specs=jax.tree.map(lambda _: vmem, outs),
             scratch_shapes=scratch,
             compiler_params=pltpu.CompilerParams(vmem_limit_bytes=24 * 2**20),
@@ -336,17 +342,15 @@
 
     shape = jax.ShapeDtypeStruct
     every = jnp.concatenate([shelter_embed, hazard, shelter_pot], axis=0)[None]
-    tile = math.gcd(rows, 1024)
     other = call(
-        functools.partial(anchors_kernel, tile),
-        shape((DEPTH, rows), bf16),
+        functools.partial(anchors_kernel, math.gcd(rows, 1024)),
+        shape((rows // 128, DEPTH, 128), bf16),
         [anchor_embed],
-        [pltpu.VMEM((emb, rows), f32), pltpu.SemaphoreType.DMA((rows // tile,))],
+        [],
         64 * rows,
-        pl.BlockSpec(memory_space=pltpu.HBM),
-    )
-
-    tile = math.gcd(half, 1024)
+    )
+
+    tile = math.gcd(half, 4096)
 
     def part(some):
         blocks = some.shape[0]
@@ -379,7 +383,7 @@
         half * columns * (groups - done),
     )
 
-    tile = math.gcd(half, 2048)
+    tile = math.gcd(half, 4096)
     state = [shape((columns, 128), f32)] * 3
     lses = [lse] + ([swapped(lse, 1, groups)] if pairs == 2 else [])
     sums = call(

time: 36.1 us -> 32.4 us (0.90)
  Pallas kernels: 21.5 us -> 16.5 us
  waiting for transfers between devices: 2.83 us -> 3.59 us
  starting transfers between devices: 7.87 us -> 8.32 us
    pallas_call x6, Pallas kernels: 21.5 us -> 16.5 us  [call(): pl.pallas_call(kernel, out_shape=outs, in_specs=[vmem] * len(ins), out_sp...]
    ppermute x4, waiting for transfers between devices: 1.67 us -> 2.43 us  [swapped(): return lax.ppermute(value, 'shel', [(k, k ^ far) for k in range(groups)])]
    ppermute x4, starting transfers between devices: 7.87 us -> 8.32 us  [swapped(): return lax.ppermute(value, 'shel', [(k, k ^ far) for k in range(groups)])]
  transfers between devices with their start and end apart: 5 -> 5, of which waited for: 2 -> 3; matrix products, arithmetic and copies ran while one was open for 0% -> 0% of each run, Pallas kernels for 34% -> 26%
where the time goes in v3:
time: 32.4 us; the launch traced here: 32.1 us
  Pallas kernels  16.5 us (51%)
  starting transfers between devices  8.32 us (26%)
  waiting for transfers between devices  3.59 us (11%)
  local copies, waits for them, and re-layouts  1.59 us (5%)
  other arithmetic  1.38 us (4%)
  between operations  0.69 us (2%)
    pallas_call x6, Pallas kernels, call(): pl.pallas_call(kernel, out_shape=outs, in_specs=[vmem] * len(ins), out_sp...  16.5 us
    ppermute x4, starting transfers between devices, swapped(): return lax.ppermute(value, 'shel', [(k, k ^ far) for k in range(groups)])  8.32 us
    ppermute x4, waiting for transfers between devices, swapped(): return lax.ppermute(value, 'shel', [(k, k ^ far) for k in range(groups)])  2.43 us
    unnamed x2, local copies, waits for them, and re-layouts  1.59 us
    ppermute x1, waiting for transfers between devices, on_device(): lax.ppermute(column, 'orig', [(k, (k + d) % halves) for k in range(halves)])  1.16 us
    broadcast_in_dim x1, other arithmetic, on_device(): every = jnp.concatenate([shelter_embed, hazard, shelter_pot], axis=0)[None]  0.76 us
  transfers between devices with their start and end apart: 5, of which 3 were waited for; matrix products, arithmetic and copies ran while one was open for 0% of the time, Pallas kernels for 26%

profile of v3, /device:TPU:0, one launch (start us, length us, event | category | flops | bytes accessed | tf_op | source)
XLA Modules:
  0.0 32.1 jit_solution(14596010854184758407)
XLA Ops:
  0.6 0.8 %maximum_bitcast_fusion = f32[1,36,128]{2,1,0:T(8,128)S(1)} fusion(f32[2,128]{1,0:T(2,128)} %param.7, f32[2,128]{1,0:T(2,128)} %param.6, f32[32,128]{1,0:T(8,128)} %param.5), kind=kLoop, calls=%fused_computation.3 | loop fusion | flops 9216 | bytes 36864 | tf_op jit(solution)/shard_map/broadcast_in_dim | solution.py:344
  1.4 3.0 %collective-permute-start = (f32[1,36,128]{2,1,0:T(8,128)S(1)}, f32[1,36,128]{2,1,0:T(8,128)S(1)}, u32[]{:S(2)}, u32[]{:S(2)}) collective-permute-start(f32[1,36,128]{2,1,0:T(8,128)S(1)} %maximum_bitcast_fusion), channel_id=1, source_target_pairs={{0,1},{1,0},{2,3},{3,2},{4,5},{5,4},{6,7},{7,6},{8,9},{9,8},{10,11... | collective-permute-start | bytes 55304 | tf_op jit(solution)/shard_map/ppermute | solution.py:315
  4.4 0.0 copy-start
  4.4 1.6 %copy-done = f32[32,16384]{1,0:T(8,128)S(1)} copy-done((f32[32,16384]{1,0:T(8,128)S(1)}, f32[32,16384]{1,0:T(8,128)}, u32[]{:S(2)}) %copy-start) | copy-done | bytes 2097176
  6.0 1.1 %shard_map.59.other_ref = bf16[128,256,128]{2,1,0:T(8,128)(2,1)S(1)} custom-call(f32[32,16384]{1,0:T(8,128)S(1)} %copy-done), custom_call_target="tpu_custom_call" | custom-call | flops 536870912 | bytes 4194304 | tf_op jit(solution)/shard_map/pallas_call | solution.py:330
  7.1 0.0 collective-permute-done
  7.1 1.6 %collective-permute-start.1 = (f32[2,36,128]{2,1,0:T(8,128)S(1)}, f32[2,36,128]{2,1,0:T(8,128)S(1)}, u32[]{:S(2)}, u32[]{:S(2)}) collective-permute-start(f32[2,36,128]{2,1,0:T(8,128)S(1)} %pad_maximum_fusion.2.z_ref), channel_id=1, source_target_pairs={{0,2},{1,3},{2,0},{3,1},{4,6},{5,7},{6,4},{7,5},{8,10},{9,11},{10,... | collective-permute-start | bytes 110600 | tf_op jit(solution)/shard_map/ppermute | solution.py:315
  8.8 2.8 %shard_map.60.refs_0_ = f32[8,8192]{1,0:T(8,128)S(1)} custom-call(bf16[128,256,128]{2,1,0:T(8,128)(2,1)S(1)} %shard_map.59.other_ref, f32[2,36,128]{2,1,0:T(8,128)S(1)} %pad_maximum_fusion.2.z_ref), custom_call_target="tpu_custom_call" | custom-call | flops 1073741824 | bytes 4194304 | tf_op jit(solution)/shard_map/pallas_call | solution.py:330
  11.6 0.0 collective-permute-done.1.z_ref
  11.6 2.7 %collective-permute-start.2 = (f32[4,36,128]{2,1,0:T(8,128)S(1)}, f32[4,36,128]{2,1,0:T(8,128)S(1)}, u32[]{:S(2)}, u32[]{:S(2)}) collective-permute-start(f32[4,36,128]{2,1,0:T(8,128)S(1)} %pad_maximum_fusion.1), channel_id=1, source_target_pairs={{0,4},{1,5},{2,6},{3,7},{4,0},{5,1},{6,2},{7,3},{8,12},{9,13},{10,... | collective-permute-start | bytes 221192 | tf_op jit(solution)/shard_map/ppermute | solution.py:315
  14.3 2.8 %shard_map.61.refs_1_ = f32[8,8192]{1,0:T(8,128)S(1)} custom-call(bf16[128,256,128]{2,1,0:T(8,128)(2,1)S(1)} %shard_map.59.other_ref, f32[2,36,128]{2,1,0:T(8,128)S(1)} %collective-permute-done.1.z_ref), custom_call_target="tpu_custom_call" | custom-call | flops 1073741824 | bytes 4194304 | tf_op jit(solution)/shard_map/pallas_call | solution.py:330
  17.1 0.8 %collective-permute-done.2 = f32[4,36,128]{2,1,0:T(8,128)S(1)} collective-permute-done((f32[4,36,128]{2,1,0:T(8,128)S(1)}, f32[4,36,128]{2,1,0:T(8,128)S(1)}, u32[]{:S(2)}, u32[]{:S(2)}) %collective-permute-start.2) | collective-permute-done | bytes 73760 | tf_op jit(solution)/shard_map/ppermute | solution.py:315
  17.9 5.5 %shard_map.62.lse_ref.refs_0_ = f32[2,8192]{1,0:T(2,128)S(1)} custom-call(bf16[128,256,128]{2,1,0:T(8,128)(2,1)S(1)} %shard_map.59.other_ref, f32[8,36,128]{2,1,0:T(8,128)S(1)} %pad_maximum_fusion.z_ref, f32[8,8192]{1,0:T(8,128)S(1)} %shard_map.60.refs_0_, f32[8,8192]{1,0:T(8,128)S(1)} %shard_map.61.refs_1_), custom_call_target="tpu_custom_call" | custom-call | flops 2147483648 | bytes 4194304 | tf_op jit(solution)/shard_map/pallas_call | solution.py:330
  23.5 1.0 %collective-permute-start.3 = (f32[2,8192]{1,0:T(2,128)S(1)}, f32[2,8192]{1,0:T(2,128)S(1)}, u32[]{:S(2)}, u32[]{:S(2)}) collective-permute-start(f32[2,8192]{1,0:T(2,128)S(1)} %shard_map.62.lse_ref.refs_0_), channel_id=1, source_target_pairs={{0,1},{1,0},{2,3},{3,2},{4,5},{5,4},{6,7},{7,6},{8,9},{9,8},{10,11... | collective-permute-start | bytes 196616 | tf_op jit(solution)/shard_map/ppermute | solution.py:315
  24.5 1.7 %shard_map.63 = (f32[128,128]{1,0:T(8,128)S(1)}, f32[128,128]{1,0:T(8,128)S(1)}, f32[128,128]{1,0:T(8,128)S(1)}) custom-call(bf16[128,256,128]{2,1,0:T(8,128)(2,1)S(1)} %shard_map.59.other_ref, f32[8,36,128]{2,1,0:T(8,128)S(1)} %pad_maximum_fusion.z_ref, f32[2,8192]{1,0:T(2,128)S(1)} %shard_map.62.lse_ref.refs_0_), custom_call_target="tpu_custom_call" | custom-call | flops 536870912 | bytes 4194304 | tf_op jit(solution)/shard_map/pallas_call | solution.py:330
  26.2 1.6 %collective-permute-done.3.refs_1_ = f32[2,8192]{1,0:T(2,128)S(1)} collective-permute-done((f32[2,8192]{1,0:T(2,128)S(1)}, f32[2,8192]{1,0:T(2,128)S(1)}, u32[]{:S(2)}, u32[]{:S(2)}) %collective-permute-start.3) | collective-permute-done | bytes 65568 | tf_op jit(solution)/shard_map/ppermute | solution.py:315
  27.8 2.5 %shard_map.64 = (f32[2,16384]{1,0:T(2,128)}, f32[2,128]{1,0:T(2,128)S(1)}) custom-call(bf16[128,256,128]{2,1,0:T(8,128)(2,1)S(1)} %shard_map.59.other_ref, f32[8,36,128]{2,1,0:T(8,128)S(1)} %pad_maximum_fusion.z_ref, f32[2,8192]{1,0:T(2,128)S(1)} %shard_map.62.lse_ref.refs_0_, f32[2,8192]{1,0:T(2,128)S(1)} %collective-permute-done.3.refs_1_, ...), custom_call_target="tpu_custom_call" | custom-call | flops 536870912 | bytes 4194304 | tf_op jit(solution)/shard_map/pallas_call | solution.py:330
  30.3 0.0 collective-permute-start.4
  30.3 1.2 %collective-permute-done.4 = f32[2,128]{1,0:T(2,128)S(1)} collective-permute-done((f32[2,128]{1,0:T(2,128)S(1)}, f32[2,128]{1,0:T(2,128)S(1)}, u32[]{:S(2)}, u32[]{:S(2)}) %collective-permute-start.4) | collective-permute-done | bytes 1056 | tf_op jit(solution)/shard_map/ppermute | solution.py:407
  31.5 0.6 %multiply_subtract_fusion = f32[2,128]{1,0:T(2,128)} fusion(f32[2,128]{1,0:T(2,128)S(1)} %collective-permute-done.4, f32[2,128]{1,0:T(2,128)S(1)} %get-tuple-element.11), kind=kLoop, calls=%fused_computation.4 | loop fusion | flops 2560 | bytes 3072 | tf_op jit(solution)/shard_map/sub | solution.py:410
  (3 shorter events, 0.0 us)
Async XLA Ops:
  1.4 5.7 %collective-permute-start = (f32[1,36,128]{2,1,0:T(8,128)S(1)}, f32[1,36,128]{2,1,0:T(8,128)S(1)}, u32[]{:S(2)}, u32[]{:S(2)}) collective-permute-start(f32[1,36,128]{2,1,0:T(8,128)S(1)} %maximum_bitcast_fusion), channel_id=1, source_target_pairs={{0,1},{1,0},{2,3},{3,2},{4,5},{5,4},{6,7},{7,6},{8,9},{9,8},{10,11... | collective-permute-start | bytes 55304 | tf_op jit(solution)/shard_map/ppermute | solution.py:315
  4.4 1.6 %copy-start = (f32[32,16384]{1,0:T(8,128)S(1)}, f32[32,16384]{1,0:T(8,128)}, u32[]{:S(2)}) copy-start(f32[32,16384]{1,0:T(8,128)} %x_ref.1) | copy-start | bytes 6291460
  7.1 4.5 %collective-permute-start.1 = (f32[2,36,128]{2,1,0:T(8,128)S(1)}, f32[2,36,128]{2,1,0:T(8,128)S(1)}, u32[]{:S(2)}, u32[]{:S(2)}) collective-permute-start(f32[2,36,128]{2,1,0:T(8,128)S(1)} %pad_maximum_fusion.2.z_ref), channel_id=1, source_target_pairs={{0,2},{1,3},{2,0},{3,1},{4,6},{5,7},{6,4},{7,5},{8,10},{9,11},{10,... | collective-permute-start | bytes 110600 | tf_op jit(solution)/shard_map/ppermute | solution.py:315
  11.6 6.3 %collective-permute-start.2 = (f32[4,36,128]{2,1,0:T(8,128)S(1)}, f32[4,36,128]{2,1,0:T(8,128)S(1)}, u32[]{:S(2)}, u32[]{:S(2)}) collective-permute-start(f32[4,36,128]{2,1,0:T(8,128)S(1)} %pad_maximum_fusion.1), channel_id=1, source_target_pairs={{0,4},{1,5},{2,6},{3,7},{4,0},{5,1},{6,2},{7,3},{8,12},{9,13},{10,... | collective-permute-start | bytes 221192 | tf_op jit(solution)/shard_map/ppermute | solution.py:315
  23.5 4.3 %collective-permute-start.3 = (f32[2,8192]{1,0:T(2,128)S(1)}, f32[2,8192]{1,0:T(2,128)S(1)}, u32[]{:S(2)}, u32[]{:S(2)}) collective-permute-start(f32[2,8192]{1,0:T(2,128)S(1)} %shard_map.62.lse_ref.refs_0_), channel_id=1, source_target_pairs={{0,1},{1,0},{2,3},{3,2},{4,5},{5,4},{6,7},{7,6},{8,9},{9,8},{10,11... | collective-permute-start | bytes 196616 | tf_op jit(solution)/shard_map/ppermute | solution.py:315
  30.3 1.2 %collective-permute-start.4 = (f32[2,128]{1,0:T(2,128)S(1)}, f32[2,128]{1,0:T(2,128)S(1)}, u32[]{:S(2)}, u32[]{:S(2)}) collective-permute-start(f32[2,128]{1,0:T(2,128)S(1)} %get-tuple-element.11), channel_id=1, source_target_pairs={{0,8},{8,0},{1,9},{9,1},{2,10},{10,2},{3,11},{11,3},{4,12},{12,4},... | collective-permute-start | bytes 3080 | tf_op jit(solution)/shard_map/ppermute | solution.py:407

commit v4 on v3

--- a/solution.py
+++ b/solution.py
@@ -10,6 +10,7 @@
 
 EPSILON = 0.25
 SCALE = math.log2(math.e) / EPSILON
+HUGE = 2.0**126
 SPREAD = 36.0
 PIECE = 512
 DEPTH = 256
@@ -165,38 +166,99 @@
     return jnp.max(jnp.abs(SCALE * ((f1 - h1) - (f0 - h0))))
 
 
+def hottest(z, side, emb):
+    columns = z.shape[1]
+    value = jnp.broadcast_to(z[emb + 2 : emb + 3] - z[emb : emb + 1], (8, columns))
+    row = lax.broadcasted_iota(jnp.int32, (8, columns), 0)
+    lane = lax.broadcasted_iota(jnp.int32, (8, columns), 1)
+    value = jnp.where(lax.rem(lane, 8) == row, value, -1e30)
+    pick = (value == jnp.max(value, axis=1, keepdims=True)).astype(jnp.float32)
+    pick = pick / jnp.sum(pick, axis=1, keepdims=True)
+    return score(pick.astype(jnp.bfloat16), side).astype(jnp.bfloat16)
+
+
 def rest_kernel(emb, tile, pairs, first, other_ref, z_ref, *refs):
-    *stats, lse_ref, side_ref, ratio_ref = refs
+    *stats, lse_ref, side_ref, ratio_ref, hot_ref = refs
     blocks, _, columns = z_ref.shape
     half = lse_ref.shape[1]
     start = starting(pairs, half)
-    for b in range(first, blocks) if blocks <= 8 else ():
+    count = side_ref.shape[0]
+    lead = hot_ref.shape[0] - min(count, 512)
+    f32 = jnp.float32
+
+    def ready(b):
         prepare(z_ref[b], emb, side_ref, ratio_ref, b - first)
-    if blocks > 8:
-
-        def ready(b, carry):
-            prepare(z_ref[b], emb, side_ref, ratio_ref, b - first)
-            return carry
-
-        lax.fori_loop(first, blocks, ready, 0)
+        side = side_ref[pl.ds((b - first) * columns, columns), :]
+        hot_ref[pl.ds((b - first) * 8, 8), :] = hottest(z_ref[b], side, emb)
+
+    if blocks <= 8:
+        for b in range(first, blocks):
+            ready(b)
+    else:
+        lax.fori_loop(first, blocks, lambda b, c: (ready(b), c)[1], 0)
+    hot_ref[lead:, :] = side_ref[: hot_ref.shape[0] - lead, :]
     near = spread_of(z_ref, emb) <= SPREAD
 
-    def step(t, carry):
+    def known(at):
+        state = None
+        for ref in stats:
+            state = merged(state, tuple(ref[k : k + 1, at] for k in range(3)))
+        return state
+
+    def store(found):
+        for at, high, *totals in found:
+            for s in range(2):
+                lse_ref[s : s + 1, at] = high + jnp.log2(totals[s])
+
+    def sums(v, shift, ratio):
+        e = jnp.exp2(v - shift)
+        w = e * wide(ratio, 256)
+        return [jnp.sum(u.reshape(u.shape[0] // 8, 8, 256), axis=0) for u in (e, w)]
+
+    def step(t, most):
         found = []
         for part in range(0, tile, 256):
             at = pl.multiple_of(t * tile + part, 256)
             other = anchors_at(other_ref, start + at, 256)
             at = pl.ds(at, 256)
-            state = one_row(all_rows(side_ref, ratio_ref, other))
-            for ref in stats:
-                state = merged(state, tuple(ref[k : k + 1, at] for k in range(3)))
-            found.append((at, state))
-        for at, state in found:
-            for s in range(2):
-                lse_ref[s : s + 1, at] = state[0] + jnp.log2(state[1 + s])
-        return carry
-
-    lax.fori_loop(0, half // tile, step, 0)
+            state = known(at)
+            v = score(hot_ref[...], other)
+            shift = jnp.max(v[:lead], axis=0, keepdims=True)
+            if state is not None:
+                shift = jnp.maximum(shift, state[0])
+            totals = sums(v[lead:], shift, ratio_ref[: count if count < 512 else 512, :])
+            if count > 512:
+
+                def more(k, totals):
+                    at = pl.ds(pl.multiple_of(k * 512, 512), 512)
+                    add = sums(score(side_ref[at, :], other), shift, ratio_ref[at, :])
+                    return [a + b for a, b in zip(totals, add)]
+
+                totals = lax.fori_loop(1, count // 512, more, totals)
+            totals = [jnp.sum(u, axis=0, keepdims=True) for u in totals]
+            if state is not None:
+                less = jnp.exp2(state[0] - shift)
+                totals = [u + w * less for u, w in zip(totals, state[1:])]
+            most = jnp.maximum(most, jnp.maximum(*totals))
+            found.append((at, shift, *totals))
+        store(found)
+        return most
+
+    most = lax.fori_loop(0, half // tile, step, jnp.zeros((1, 256), f32))
+    good = jnp.max(jnp.where(most < HUGE, 0.0, 1.0)) == 0.0
+
+    @pl.when(near & jnp.logical_not(good))
+    def _():
+        def again(t, carry):
+            at = pl.multiple_of(t * 256, 256)
+            state = one_row(all_rows(side_ref, ratio_ref, anchors_at(other_ref, start + at, 256)))
+            at = pl.ds(at, 256)
+            if stats:
+                state = merged(known(at), state)
+            store([(at, *state)])
+            return carry
+
+        lax.fori_loop(0, half // 256, again, 0)
 
     @pl.when(jnp.logical_not(near))
     def _():
@@ -264,13 +326,19 @@
 
 def finish_kernel(emb, tile, pairs, shelters, other_ref, z_ref, *refs):
     lse_refs, refs = refs[:pairs], refs[pairs:]
-    *old, anchor_ref, column_ref, top_ref, sum0_ref, sum1_ref, side_ref = refs
+    *old, anchor_hbm, column_ref, top_ref, sum0_ref, sum1_ref, side_ref, anchor_ref, sems = refs
     half = lse_refs[0].shape[1]
     mine = lax.rem(lax.axis_index("shel"), pairs)
     near = spread_of(z_ref, emb) <= SPREAD
     starts = [pl.multiple_of((mine ^ k) * half, half) for k in range(pairs)]
     side_ref[...] = y_side(z_ref[0], emb)
     states = (top_ref, sum0_ref, sum1_ref)
+    writes = []
+    for k, (start, lse_ref) in enumerate(zip(starts, lse_refs)):
+        at = pl.ds(start, half)
+        anchor_ref[:, at] = (-EPSILON * math.log(shelters)) - (EPSILON * math.log(2.0)) * lse_ref[...]
+        writes.append(pltpu.make_async_copy(anchor_ref.at[:, at], anchor_hbm.at[:, at], sems.at[k]))
+        writes[-1].start()
     for new, ref in zip(states, old):
         new[...] = ref[...]
     for start, lse_ref in list(zip(starts, lse_refs))[1:]:
@@ -287,8 +355,6 @@
 
     for s, v in enumerate(one(*(ref[...] for ref in states))):
         column_ref[s : s + 1, :] = v + offset[s]
-    for start, lse_ref in zip(starts, lse_refs):
-        anchor_ref[:, pl.ds(start, half)] = (-EPSILON * math.log(shelters)) - (EPSILON * math.log(2.0)) * lse_ref[...]
 
     @pl.when(jnp.logical_not(near))
     def _():
@@ -309,6 +375,9 @@
 
                 lax.fori_loop(0, half // 256, column, 0)
             column_ref[s : s + 1, :] = one(top_ref[...], sum0_ref[...])[0] + offset[s]
+
+    for write in writes:
+        write.wait()
 
 
 def swapped(value, far, groups):
@@ -326,12 +395,12 @@
     f32, bf16 = jnp.float32, jnp.bfloat16
     vmem = pl.BlockSpec(memory_space=pltpu.VMEM)
 
-    def call(kernel, outs, ins, scratch, work):
+    def call(kernel, outs, ins, scratch, work, places=None):
         return pl.pallas_call(
             kernel,
             out_shape=outs,
             in_specs=[vmem] * len(ins),
-            out_specs=jax.tree.map(lambda _: vmem, outs),
+            out_specs=places or jax.tree.map(lambda _: vmem, outs),
             scratch_shapes=scratch,
             compiler_params=pltpu.CompilerParams(vmem_limit_bytes=24 * 2**20),
             cost_estimate=pl.CostEstimate(flops=2 * DEPTH * work, bytes_accessed=DEPTH * rows, transcendentals=work),
@@ -364,14 +433,14 @@
 
     stats, done = [], 0
     if groups & (groups - 1) == 0:
-        far = 1
-        while far < groups:
+        far = groups // 2
+        while far:
             got = swapped(every, far, groups)
-            if far > 1:
+            if every.shape[0] > 1:
                 stats.append(part(every[done:]))
-                done = far
+                done = every.shape[0]
             every = jnp.concatenate([every, got], axis=0)
-            far *= 2
+            far //= 2
     else:
         blocks = [lax.ppermute(every, "shel", [(k, (k + d) % groups) for k in range(groups)]) for d in range(1, groups)]
         every = jnp.concatenate([every, *blocks])
@@ -379,7 +448,7 @@
         functools.partial(rest_kernel, emb, tile, pairs, done),
         shape((2, half), f32),
         [other, every, *stats],
-        sides(groups - done),
+        [*sides(groups - done), pltpu.VMEM((8 * (groups - done) + min(512, (groups - done) * columns), DEPTH), bf16)],
         half * columns * (groups - done),
     )
 
@@ -397,8 +466,10 @@
         functools.partial(finish_kernel, emb, tile, pairs, shelters),
         (shape((2, rows), f32), shape((2, columns), f32)),
         [other, every, *lses, *sums],
-        [pltpu.VMEM(s.shape, f32) for s in state] + [pltpu.VMEM((columns, DEPTH), bf16)],
+        [pltpu.VMEM(s.shape, f32) for s in state]
+        + [pltpu.VMEM((columns, DEPTH), bf16), pltpu.VMEM((2, rows), f32), pltpu.SemaphoreType.DMA((pairs,))],
         half * columns,
+        (pl.BlockSpec(memory_space=pl.ANY), vmem),
     )
 
     halves = lax.axis_size("orig")

time: 32.4 us -> 30 us (0.926)
  Pallas kernels: 16.5 us -> 14.8 us
  waiting for transfers between devices: 3.59 us -> 2.3 us
  starting transfers between devices: 8.32 us -> 8.95 us
    pallas_call x6, Pallas kernels: 16.5 us -> 14.8 us  [call(): pl.pallas_call(kernel, out_shape=outs, in_specs=[vmem] * len(ins), out_sp...]
    ppermute x4, waiting for transfers between devices: 2.43 us -> 1.15 us  [swapped(): return lax.ppermute(value, 'shel', [(k, k ^ far) for k in range(groups)])]
    ppermute x4, starting transfers between devices: 8.32 us -> 8.87 us  [swapped(): return lax.ppermute(value, 'shel', [(k, k ^ far) for k in range(groups)])]
  transfers between devices with their start and end apart: 5 -> 5, of which waited for: 3 -> 3; matrix products, arithmetic and copies ran while one was open for 0% -> 0% of each run, Pallas kernels for 26% -> 29%
where the time goes in v4:
time: 30 us; the launch traced here: 29.7 us
  Pallas kernels  14.8 us (49%)
  starting transfers between devices  8.95 us (30%)
  waiting for transfers between devices  2.3 us (8%)
  local copies, waits for them, and re-layouts  1.59 us (5%)
  other arithmetic  1.38 us (5%)
  between operations  0.7 us (2%)
    pallas_call x6, Pallas kernels, call(): pl.pallas_call(kernel, out_shape=outs, in_specs=[vmem] * len(ins), out_sp...  14.8 us
    ppermute x4, starting transfers between devices, swapped(): return lax.ppermute(value, 'shel', [(k, k ^ far) for k in range(groups)])  8.87 us
    unnamed x2, local copies, waits for them, and re-layouts  1.59 us
    ppermute x4, waiting for transfers between devices, swapped(): return lax.ppermute(value, 'shel', [(k, k ^ far) for k in range(groups)])  1.15 us
    ppermute x1, waiting for transfers between devices, on_device(): lax.ppermute(column, 'orig', [(k, (k + d) % halves) for k in range(halves)])  1.15 us
    broadcast_in_dim x1, other arithmetic, on_device(): every = jnp.concatenate([shelter_embed, hazard, shelter_pot], axis=0)[None]  0.76 us
  transfers between devices with their start and end apart: 5, of which 3 were waited for; matrix products, arithmetic and copies ran while one was open for 0% of the time, Pallas kernels for 29%

profile of v4, /device:TPU:0, one launch (start us, length us, event | category | flops | bytes accessed | tf_op | source)
XLA Modules:
  0.0 29.7 jit_solution(10614969567385031305)
XLA Ops:
  0.6 0.8 %maximum_bitcast_fusion = f32[1,36,128]{2,1,0:T(8,128)S(1)} fusion(f32[2,128]{1,0:T(2,128)} %param.7, f32[2,128]{1,0:T(2,128)} %param.6, f32[32,128]{1,0:T(8,128)} %param.5), kind=kLoop, calls=%fused_computation.3 | loop fusion | flops 9216 | bytes 36864 | tf_op jit(solution)/shard_map/broadcast_in_dim | solution.py:413
  1.4 4.1 %collective-permute-start = (f32[1,36,128]{2,1,0:T(8,128)S(1)}, f32[1,36,128]{2,1,0:T(8,128)S(1)}, u32[]{:S(2)}, u32[]{:S(2)}) collective-permute-start(f32[1,36,128]{2,1,0:T(8,128)S(1)} %maximum_bitcast_fusion), channel_id=1, source_target_pairs={{0,4},{1,5},{2,6},{3,7},{4,0},{5,1},{6,2},{7,3},{8,12},{9,13},{10,... | collective-permute-start | bytes 55304 | tf_op jit(solution)/shard_map/ppermute | solution.py:384
  5.5 0.0 copy-start
  5.5 1.6 %copy-done = f32[32,16384]{1,0:T(8,128)S(1)} copy-done((f32[32,16384]{1,0:T(8,128)S(1)}, f32[32,16384]{1,0:T(8,128)}, u32[]{:S(2)}) %copy-start) | copy-done | bytes 2097176
  7.0 1.1 %shard_map.59.other_ref = bf16[128,256,128]{2,1,0:T(8,128)(2,1)S(1)} custom-call(f32[32,16384]{1,0:T(8,128)S(1)} %copy-done), custom_call_target="tpu_custom_call" | custom-call | flops 536870912 | bytes 4194304 | tf_op jit(solution)/shard_map/pallas_call | solution.py:399
  8.2 0.0 collective-permute-done
  8.2 1.6 %collective-permute-start.1 = (f32[2,36,128]{2,1,0:T(8,128)S(1)}, f32[2,36,128]{2,1,0:T(8,128)S(1)}, u32[]{:S(2)}, u32[]{:S(2)}) collective-permute-start(f32[2,36,128]{2,1,0:T(8,128)S(1)} %pad_maximum_fusion.2.z_ref), channel_id=1, source_target_pairs={{0,2},{1,3},{2,0},{3,1},{4,6},{5,7},{6,4},{7,5},{8,10},{9,11},{10,... | collective-permute-start | bytes 110600 | tf_op jit(solution)/shard_map/ppermute | solution.py:384
  9.9 2.8 %shard_map.60.refs_0_ = f32[8,8192]{1,0:T(8,128)S(1)} custom-call(bf16[128,256,128]{2,1,0:T(8,128)(2,1)S(1)} %shard_map.59.other_ref, f32[2,36,128]{2,1,0:T(8,128)S(1)} %pad_maximum_fusion.2.z_ref), custom_call_target="tpu_custom_call" | custom-call | flops 1073741824 | bytes 4194304 | tf_op jit(solution)/shard_map/pallas_call | solution.py:399
  12.7 0.0 collective-permute-done.1.z_ref
  12.7 1.6 %collective-permute-start.2 = (f32[4,36,128]{2,1,0:T(8,128)S(1)}, f32[4,36,128]{2,1,0:T(8,128)S(1)}, u32[]{:S(2)}, u32[]{:S(2)}) collective-permute-start(f32[4,36,128]{2,1,0:T(8,128)S(1)} %pad_maximum_fusion.1), channel_id=1, source_target_pairs={{0,1},{1,0},{2,3},{3,2},{4,5},{5,4},{6,7},{7,6},{8,9},{9,8},{10,11... | collective-permute-start | bytes 221192 | tf_op jit(solution)/shard_map/ppermute | solution.py:384
  14.3 2.8 %shard_map.61.refs_1_ = f32[8,8192]{1,0:T(8,128)S(1)} custom-call(bf16[128,256,128]{2,1,0:T(8,128)(2,1)S(1)} %shard_map.59.other_ref, f32[2,36,128]{2,1,0:T(8,128)S(1)} %collective-permute-done.1.z_ref), custom_call_target="tpu_custom_call" | custom-call | flops 1073741824 | bytes 4194304 | tf_op jit(solution)/shard_map/pallas_call | solution.py:399
  17.1 0.1 collective-permute-done.2
  17.2 4.5 %shard_map.62.lse_ref.refs_0_ = f32[2,8192]{1,0:T(2,128)S(1)} custom-call(bf16[128,256,128]{2,1,0:T(8,128)(2,1)S(1)} %shard_map.59.other_ref, f32[8,36,128]{2,1,0:T(8,128)S(1)} %pad_maximum_fusion.z_ref, f32[8,8192]{1,0:T(8,128)S(1)} %shard_map.60.refs_0_, f32[8,8192]{1,0:T(8,128)S(1)} %shard_map.61.refs_1_), custom_call_target="tpu_custom_call" | custom-call | flops 2147483648 | bytes 4194304 | tf_op jit(solution)/shard_map/pallas_call | solution.py:399
  21.7 1.6 %collective-permute-start.3 = (f32[2,8192]{1,0:T(2,128)S(1)}, f32[2,8192]{1,0:T(2,128)S(1)}, u32[]{:S(2)}, u32[]{:S(2)}) collective-permute-start(f32[2,8192]{1,0:T(2,128)S(1)} %shard_map.62.lse_ref.refs_0_), channel_id=1, source_target_pairs={{0,1},{1,0},{2,3},{3,2},{4,5},{5,4},{6,7},{7,6},{8,9},{9,8},{10,11... | collective-permute-start | bytes 196616 | tf_op jit(solution)/shard_map/ppermute | solution.py:384
  23.3 1.7 %shard_map.63 = (f32[128,128]{1,0:T(8,128)S(1)}, f32[128,128]{1,0:T(8,128)S(1)}, f32[128,128]{1,0:T(8,128)S(1)}) custom-call(bf16[128,256,128]{2,1,0:T(8,128)(2,1)S(1)} %shard_map.59.other_ref, f32[8,36,128]{2,1,0:T(8,128)S(1)} %pad_maximum_fusion.z_ref, f32[2,8192]{1,0:T(2,128)S(1)} %shard_map.62.lse_ref.refs_0_), custom_call_target="tpu_custom_call" | custom-call | flops 536870912 | bytes 4194304 | tf_op jit(solution)/shard_map/pallas_call | solution.py:399
  25.0 1.1 %collective-permute-done.3.refs_1_ = f32[2,8192]{1,0:T(2,128)S(1)} collective-permute-done((f32[2,8192]{1,0:T(2,128)S(1)}, f32[2,8192]{1,0:T(2,128)S(1)}, u32[]{:S(2)}, u32[]{:S(2)}) %collective-permute-start.3) | collective-permute-done | bytes 65568 | tf_op jit(solution)/shard_map/ppermute | solution.py:384
  26.0 1.9 %shard_map.64 = (f32[2,16384]{1,0:T(2,128)}, f32[2,128]{1,0:T(2,128)S(1)}) custom-call(bf16[128,256,128]{2,1,0:T(8,128)(2,1)S(1)} %shard_map.59.other_ref, f32[8,36,128]{2,1,0:T(8,128)S(1)} %pad_maximum_fusion.z_ref, f32[2,8192]{1,0:T(2,128)S(1)} %shard_map.62.lse_ref.refs_0_, f32[2,8192]{1,0:T(2,128)S(1)} %collective-permute-done.3.refs_1_, ...), custom_call_target="tpu_custom_call" | custom-call | flops 536870912 | bytes 4194304 | tf_op jit(solution)/shard_map/pallas_call | solution.py:399
  27.9 0.1 collective-permute-start.4
  28.0 1.1 %collective-permute-done.4 = f32[2,128]{1,0:T(2,128)S(1)} collective-permute-done((f32[2,128]{1,0:T(2,128)S(1)}, f32[2,128]{1,0:T(2,128)S(1)}, u32[]{:S(2)}, u32[]{:S(2)}) %collective-permute-start.4) | collective-permute-done | bytes 1056 | tf_op jit(solution)/shard_map/ppermute | solution.py:478
  29.2 0.6 %multiply_subtract_fusion = f32[2,128]{1,0:T(2,128)} fusion(f32[2,128]{1,0:T(2,128)S(1)} %collective-permute-done.4, f32[2,128]{1,0:T(2,128)S(1)} %get-tuple-element.11), kind=kLoop, calls=%fused_computation.4 | loop fusion | flops 2560 | bytes 3072 | tf_op jit(solution)/shard_map/sub | solution.py:481
  (3 shorter events, 0.0 us)
Async XLA Ops:
  1.4 6.8 %collective-permute-start = (f32[1,36,128]{2,1,0:T(8,128)S(1)}, f32[1,36,128]{2,1,0:T(8,128)S(1)}, u32[]{:S(2)}, u32[]{:S(2)}) collective-permute-start(f32[1,36,128]{2,1,0:T(8,128)S(1)} %maximum_bitcast_fusion), channel_id=1, source_target_pairs={{0,4},{1,5},{2,6},{3,7},{4,0},{5,1},{6,2},{7,3},{8,12},{9,13},{10,... | collective-permute-start | bytes 55304 | tf_op jit(solution)/shard_map/ppermute | solution.py:384
  5.5 1.6 %copy-start = (f32[32,16384]{1,0:T(8,128)S(1)}, f32[32,16384]{1,0:T(8,128)}, u32[]{:S(2)}) copy-start(f32[32,16384]{1,0:T(8,128)} %x_ref.1) | copy-start | bytes 6291460
  8.2 4.5 %collective-permute-start.1 = (f32[2,36,128]{2,1,0:T(8,128)S(1)}, f32[2,36,128]{2,1,0:T(8,128)S(1)}, u32[]{:S(2)}, u32[]{:S(2)}) collective-permute-start(f32[2,36,128]{2,1,0:T(8,128)S(1)} %pad_maximum_fusion.2.z_ref), channel_id=1, source_target_pairs={{0,2},{1,3},{2,0},{3,1},{4,6},{5,7},{6,4},{7,5},{8,10},{9,11},{10,... | collective-permute-start | bytes 110600 | tf_op jit(solution)/shard_map/ppermute | solution.py:384
  12.7 4.5 %collective-permute-start.2 = (f32[4,36,128]{2,1,0:T(8,128)S(1)}, f32[4,36,128]{2,1,0:T(8,128)S(1)}, u32[]{:S(2)}, u32[]{:S(2)}) collective-permute-start(f32[4,36,128]{2,1,0:T(8,128)S(1)} %pad_maximum_fusion.1), channel_id=1, source_target_pairs={{0,1},{1,0},{2,3},{3,2},{4,5},{5,4},{6,7},{7,6},{8,9},{9,8},{10,11... | collective-permute-start | bytes 221192 | tf_op jit(solution)/shard_map/ppermute | solution.py:384
  21.7 4.3 %collective-permute-start.3 = (f32[2,8192]{1,0:T(2,128)S(1)}, f32[2,8192]{1,0:T(2,128)S(1)}, u32[]{:S(2)}, u32[]{:S(2)}) collective-permute-start(f32[2,8192]{1,0:T(2,128)S(1)} %shard_map.62.lse_ref.refs_0_), channel_id=1, source_target_pairs={{0,1},{1,0},{2,3},{3,2},{4,5},{5,4},{6,7},{7,6},{8,9},{9,8},{10,11... | collective-permute-start | bytes 196616 | tf_op jit(solution)/shard_map/ppermute | solution.py:384
  27.9 1.2 %collective-permute-start.4 = (f32[2,128]{1,0:T(2,128)S(1)}, f32[2,128]{1,0:T(2,128)S(1)}, u32[]{:S(2)}, u32[]{:S(2)}) collective-permute-start(f32[2,128]{1,0:T(2,128)S(1)} %get-tuple-element.11), channel_id=1, source_target_pairs={{0,8},{8,0},{1,9},{9,1},{2,10},{10,2},{3,11},{11,3},{4,12},{12,4},... | collective-permute-start | bytes 3080 | tf_op jit(solution)/shard_map/ppermute | solution.py:478

commit v5 on v4

--- a/solution.py
+++ b/solution.py
@@ -130,8 +130,19 @@
     return pl.multiple_of(lax.rem(lax.axis_index("shel"), pairs) * half, half)
 
 
-def anchors_kernel(tile, x_ref, other_ref):
+def anchors_kernel(tile, x_hbm, other_ref, x_ref, sems):
+    def fetch(t):
+        at = pl.ds(pl.multiple_of(t * tile, tile), tile)
+        return pltpu.make_async_copy(x_hbm.at[:, at], x_ref.at[:, at], sems.at[t])
+
+    def begin(t, carry):
+        fetch(t).start()
+        return carry
+
+    lax.fori_loop(0, x_ref.shape[1] // tile, begin, 0)
+
     def step(t, carry):
+        fetch(t).wait()
         side = x_side(x_ref[:, pl.ds(pl.multiple_of(t * tile, tile), tile)])
         for k in range(tile // 128):
             other_ref[t * (tile // 128) + k] = side[:, k * 128 : (k + 1) * 128]
@@ -285,8 +296,8 @@
             lax.fori_loop(0, half // 256, exact, 0)
 
 
-def column_sums(side, other_ref, start, lse_ref, tile, state_refs):
-    columns = side.shape[0]
+def column_sums(scores_at, lse_ref, tile, state_refs):
+    columns = state_refs[0].shape[0]
     piece = math.gcd(tile, PIECE)
 
     def some(at, v):
@@ -307,7 +318,7 @@
 
     def step(t, carry):
         ats = [pl.multiple_of(t * tile + k, piece) for k in range(0, tile, piece)]
-        scores = [score(side, anchors_at(other_ref, start + at, piece)) for at in ats]
+        scores = [scores_at(at, piece) for at in ats]
         for at, v in zip(ats, scores):
             some(at, v)
         return carry
@@ -315,23 +326,37 @@
     lax.fori_loop(0, lse_ref.shape[1] // tile, step, 0)
 
 
-def columns_kernel(emb, tile, pairs, other_ref, z_ref, lse_ref, top_ref, sum0_ref, sum1_ref, side_ref):
+def columns_kernel(emb, tile, pairs, other_ref, z_ref, lse_ref, top_ref, sum0_ref, sum1_ref, *refs):
+    *later, side_ref = refs
     half = lse_ref.shape[1]
+    start = starting(pairs, half)
     side_ref[...] = y_side(z_ref[0], emb)
     top_ref[...] = jnp.full(top_ref.shape, -1e30, jnp.float32)
     sum0_ref[...] = jnp.zeros(sum0_ref.shape, jnp.float32)
     sum1_ref[...] = jnp.zeros(sum1_ref.shape, jnp.float32)
-    column_sums(side_ref[...], other_ref, starting(pairs, half), lse_ref, tile, (top_ref, sum0_ref, sum1_ref))
+
+    def scores_at(at, width):
+        return score(side_ref[...], anchors_at(other_ref, start + at, width))
+
+    column_sums(scores_at, lse_ref, tile, (top_ref, sum0_ref, sum1_ref))
+    if later:
+
+        def step(t, carry):
+            for part in range(0, tile, 256):
+                at = pl.multiple_of(t * tile + part, 256)
+                later[0][:, pl.ds(at, 256)] = score(side_ref[...], anchors_at(other_ref, half - start + at, 256))
+            return carry
+
+        lax.fori_loop(0, half // tile, step, 0)
 
 
 def finish_kernel(emb, tile, pairs, shelters, other_ref, z_ref, *refs):
-    lse_refs, refs = refs[:pairs], refs[pairs:]
+    lse_refs, scores, refs = refs[:pairs], refs[pairs : 2 * pairs - 1], refs[2 * pairs - 1 :]
     *old, anchor_hbm, column_ref, top_ref, sum0_ref, sum1_ref, side_ref, anchor_ref, sems = refs
     half = lse_refs[0].shape[1]
     mine = lax.rem(lax.axis_index("shel"), pairs)
     near = spread_of(z_ref, emb) <= SPREAD
     starts = [pl.multiple_of((mine ^ k) * half, half) for k in range(pairs)]
-    side_ref[...] = y_side(z_ref[0], emb)
     states = (top_ref, sum0_ref, sum1_ref)
     writes = []
     for k, (start, lse_ref) in enumerate(zip(starts, lse_refs)):
@@ -341,8 +366,8 @@
         writes[-1].start()
     for new, ref in zip(states, old):
         new[...] = ref[...]
-    for start, lse_ref in list(zip(starts, lse_refs))[1:]:
-        column_sums(side_ref[...], other_ref, start, lse_ref, tile, states)
+    for score_ref, lse_ref in zip(scores, lse_refs[1:]):
+        column_sums(lambda at, width: score_ref[:, pl.ds(at, width)], lse_ref, tile, states)
     z = z_ref[0]
     h0, h1, f0, f1 = (z[emb + k : emb + k + 1] for k in range(4))
     offset = (-SCALE * f0 - math.log2(shelters), -SCALE * (h1 + f0 - h0) - math.log2(shelters))
@@ -358,6 +383,7 @@
 
     @pl.when(jnp.logical_not(near))
     def _():
+        side_ref[...] = y_side(z_ref[0], emb)
         for s in range(2):
             top_ref[...] = jnp.full(top_ref.shape, -1e30, jnp.float32)
             sum0_ref[...] = jnp.zeros(sum0_ref.shape, jnp.float32)
@@ -395,11 +421,11 @@
     f32, bf16 = jnp.float32, jnp.bfloat16
     vmem = pl.BlockSpec(memory_space=pltpu.VMEM)
 
-    def call(kernel, outs, ins, scratch, work, places=None):
+    def call(kernel, outs, ins, scratch, work, places=None, first=None):
         return pl.pallas_call(
             kernel,
             out_shape=outs,
-            in_specs=[vmem] * len(ins),
+            in_specs=[first or vmem] + [vmem] * (len(ins) - 1),
             out_specs=places or jax.tree.map(lambda _: vmem, outs),
             scratch_shapes=scratch,
             compiler_params=pltpu.CompilerParams(vmem_limit_bytes=24 * 2**20),
@@ -414,9 +440,10 @@
     other = call(
         functools.partial(anchors_kernel, math.gcd(rows, 1024)),
         shape((rows // 128, DEPTH, 128), bf16),
-        [anchor_embed],
-        [],
+        [pltpu.with_memory_space_constraint(anchor_embed, pltpu.HBM)],
+        [pltpu.VMEM((emb, rows), f32), pltpu.SemaphoreType.DMA((rows // math.gcd(rows, 1024),))],
         64 * rows,
+        first=pl.BlockSpec(memory_space=pltpu.HBM),
     )
 
     tile = math.gcd(half, 4096)
@@ -455,17 +482,19 @@
     tile = math.gcd(half, 4096)
     state = [shape((columns, 128), f32)] * 3
     lses = [lse] + ([swapped(lse, 1, groups)] if pairs == 2 else [])
-    sums = call(
+    later = [shape((columns, half), f32)] * (pairs - 1)
+    found = call(
         functools.partial(columns_kernel, emb, tile, pairs),
-        state,
+        state + later,
         [other, every, lse],
         [pltpu.VMEM((columns, DEPTH), bf16)],
-        half * columns,
+        half * columns * pairs,
     )
+    sums, scores = found[:3], found[3:]
     anchor_pot, column = call(
         functools.partial(finish_kernel, emb, tile, pairs, shelters),
         (shape((2, rows), f32), shape((2, columns), f32)),
-        [other, every, *lses, *sums],
+        [other, every, *lses, *scores, *sums],
         [pltpu.VMEM(s.shape, f32) for s in state]
         + [pltpu.VMEM((columns, DEPTH), bf16), pltpu.VMEM((2, rows), f32), pltpu.SemaphoreType.DMA((pairs,))],
         half * columns,

time: 30 us -> 29.3 us (0.977)
  Pallas kernels: 14.8 us -> 16.8 us
  local copies, waits for them, and re-layouts: 1.59 us -> 0 us
  waiting for transfers between devices: 2.3 us -> 1.23 us
    pallas_call x6, Pallas kernels: 14.8 us -> 16.8 us  [call(): pl.pallas_call(kernel, out_shape=outs, in_specs=[first or vmem] + [vmem]...]
    unnamed x2 -> x0, local copies, waits for them, and re-layouts: 1.59 us -> none
    ppermute x4, waiting for transfers between devices: 1.15 us -> 0.08 us  [swapped(): return lax.ppermute(value, 'shel', [(k, k ^ far) for k in range(groups)])]
  transfers between devices with their start and end apart: 5 -> 5, of which waited for: 3 -> 2; matrix products, arithmetic and copies ran while one was open for 0% -> 0% of each run, Pallas kernels for 29% -> 37%
where the time goes in v5:
time: 29.3 us; the launch traced here: 29 us
  Pallas kernels  16.8 us (57%)
  starting transfers between devices  8.9 us (30%)
  other arithmetic  1.38 us (5%)
  waiting for transfers between devices  1.23 us (4%)
  between operations  0.72 us (2%)
    pallas_call x6, Pallas kernels, call(): pl.pallas_call(kernel, out_shape=outs, in_specs=[first or vmem] + [vmem]...  16.8 us
    ppermute x4, starting transfers between devices, swapped(): return lax.ppermute(value, 'shel', [(k, k ^ far) for k in range(groups)])  8.83 us
    ppermute x1, waiting for transfers between devices, on_device(): lax.ppermute(column, 'orig', [(k, (k + d) % halves) for k in range(halves)])  1.15 us
    broadcast_in_dim x1, other arithmetic, on_device(): every = jnp.concatenate([shelter_embed, hazard, shelter_pot], axis=0)[None]  0.76 us
    sub x1, other arithmetic, on_device(): -EPSILON * math.log(anchors)  0.59 us
  transfers between devices with their start and end apart: 5, of which 2 were waited for; matrix products, arithmetic and copies ran while one was open for 0% of the time, Pallas kernels for 37%

profile of v5, /device:TPU:0, one launch (start us, length us, event | category | flops | bytes accessed | tf_op | source)
XLA Modules:
  0.0 29.0 jit_solution(6692813150714072683)
XLA Ops:
  0.6 0.8 %maximum_bitcast_fusion = f32[1,36,128]{2,1,0:T(8,128)S(1)} fusion(f32[2,128]{1,0:T(2,128)} %param.7, f32[2,128]{1,0:T(2,128)} %param.6, f32[32,128]{1,0:T(8,128)} %param.5), kind=kLoop, calls=%fused_computation.3 | loop fusion | flops 9216 | bytes 36864 | tf_op jit(solution)/shard_map/broadcast_in_dim | solution.py:439
  1.4 4.1 %collective-permute-start = (f32[1,36,128]{2,1,0:T(8,128)S(1)}, f32[1,36,128]{2,1,0:T(8,128)S(1)}, u32[]{:S(2)}, u32[]{:S(2)}) collective-permute-start(f32[1,36,128]{2,1,0:T(8,128)S(1)} %maximum_bitcast_fusion), channel_id=1, source_target_pairs={{0,4},{1,5},{2,6},{3,7},{4,0},{5,1},{6,2},{7,3},{8,12},{9,13},{10,... | collective-permute-start | bytes 55304 | tf_op jit(solution)/shard_map/ppermute | solution.py:410
  5.5 2.2 %shard_map.59.other_ref = bf16[128,256,128]{2,1,0:T(8,128)(2,1)S(1)} custom-call(f32[32,16384]{1,0:T(8,128)} %x_hbm.1), custom_call_target="tpu_custom_call" | custom-call | flops 536870912 | bytes 4194304 | tf_op jit(solution)/shard_map/pallas_call | solution.py:425
  7.7 0.0 collective-permute-done
  7.7 1.6 %collective-permute-start.1 = (f32[2,36,128]{2,1,0:T(8,128)S(1)}, f32[2,36,128]{2,1,0:T(8,128)S(1)}, u32[]{:S(2)}, u32[]{:S(2)}) collective-permute-start(f32[2,36,128]{2,1,0:T(8,128)S(1)} %pad_maximum_fusion.2.z_ref), channel_id=1, source_target_pairs={{0,2},{1,3},{2,0},{3,1},{4,6},{5,7},{6,4},{7,5},{8,10},{9,11},{10,... | collective-permute-start | bytes 110600 | tf_op jit(solution)/shard_map/ppermute | solution.py:410
  9.3 3.0 %shard_map.60.refs_0_ = f32[8,8192]{1,0:T(8,128)S(1)} custom-call(bf16[128,256,128]{2,1,0:T(8,128)(2,1)S(1)} %shard_map.59.other_ref, f32[2,36,128]{2,1,0:T(8,128)S(1)} %pad_maximum_fusion.2.z_ref), custom_call_target="tpu_custom_call" | custom-call | flops 1073741824 | bytes 4194304 | tf_op jit(solution)/shard_map/pallas_call | solution.py:425
  12.3 0.0 collective-permute-done.1.z_ref
  12.3 1.6 %collective-permute-start.2 = (f32[4,36,128]{2,1,0:T(8,128)S(1)}, f32[4,36,128]{2,1,0:T(8,128)S(1)}, u32[]{:S(2)}, u32[]{:S(2)}) collective-permute-start(f32[4,36,128]{2,1,0:T(8,128)S(1)} %pad_maximum_fusion.1), channel_id=1, source_target_pairs={{0,1},{1,0},{2,3},{3,2},{4,5},{5,4},{6,7},{7,6},{8,9},{9,8},{10,11... | collective-permute-start | bytes 221192 | tf_op jit(solution)/shard_map/ppermute | solution.py:410
  13.9 3.0 %shard_map.61.refs_1_ = f32[8,8192]{1,0:T(8,128)S(1)} custom-call(bf16[128,256,128]{2,1,0:T(8,128)(2,1)S(1)} %shard_map.59.other_ref, f32[2,36,128]{2,1,0:T(8,128)S(1)} %collective-permute-done.1.z_ref), custom_call_target="tpu_custom_call" | custom-call | flops 1073741824 | bytes 4194304 | tf_op jit(solution)/shard_map/pallas_call | solution.py:425
  16.9 0.0 collective-permute-done.2
  16.9 4.5 %shard_map.62.lse_ref.refs_0_ = f32[2,8192]{1,0:T(2,128)S(1)} custom-call(bf16[128,256,128]{2,1,0:T(8,128)(2,1)S(1)} %shard_map.59.other_ref, f32[8,36,128]{2,1,0:T(8,128)S(1)} %pad_maximum_fusion.z_ref, f32[8,8192]{1,0:T(8,128)S(1)} %shard_map.60.refs_0_, f32[8,8192]{1,0:T(8,128)S(1)} %shard_map.61.refs_1_), custom_call_target="tpu_custom_call" | custom-call | flops 2147483648 | bytes 4194304 | tf_op jit(solution)/shard_map/pallas_call | solution.py:425
  21.4 1.5 %collective-permute-start.3 = (f32[2,8192]{1,0:T(2,128)S(1)}, f32[2,8192]{1,0:T(2,128)S(1)}, u32[]{:S(2)}, u32[]{:S(2)}) collective-permute-start(f32[2,8192]{1,0:T(2,128)S(1)} %shard_map.62.lse_ref.refs_0_), channel_id=1, source_target_pairs={{0,1},{1,0},{2,3},{3,2},{4,5},{5,4},{6,7},{7,6},{8,9},{9,8},{10,11... | collective-permute-start | bytes 196616 | tf_op jit(solution)/shard_map/ppermute | solution.py:410
  23.0 2.7 %shard_map.63 = (f32[128,128]{1,0:T(8,128)S(1)}, f32[128,128]{1,0:T(8,128)S(1)}, f32[128,128]{1,0:T(8,128)S(1)}, f32[128,8192]{1,0:T(8,128)S(1)}) custom-call(bf16[128,256,128]{2,1,0:T(8,128)(2,1)S(1)} %shard_map.59.other_ref, f32[8,36,128]{2,1,0:T(8,128)S(1)} %pad_maximum_fusion.z_ref, f32[2,8192]{1,0:T(2,128)S(1)} %shard_map.62.lse_ref.refs_0_), custom_call_target="tpu_custom_call" | custom-call | flops 1073741824 | bytes 4194304 | tf_op jit(solution)/shard_map/pallas_call | solution.py:425
  25.7 0.1 collective-permute-done.3.refs_1_
  25.8 1.4 %shard_map.64 = (f32[2,16384]{1,0:T(2,128)}, f32[2,128]{1,0:T(2,128)S(1)}) custom-call(bf16[128,256,128]{2,1,0:T(8,128)(2,1)S(1)} %shard_map.59.other_ref, f32[8,36,128]{2,1,0:T(8,128)S(1)} %pad_maximum_fusion.z_ref, f32[2,8192]{1,0:T(2,128)S(1)} %shard_map.62.lse_ref.refs_0_, f32[2,8192]{1,0:T(2,128)S(1)} %collective-permute-done.3.refs_1_, ...), custom_call_target="tpu_custom_call" | custom-call | flops 536870912 | bytes 4194304 | tf_op jit(solution)/shard_map/pallas_call | solution.py:425
  27.2 0.1 collective-permute-start.4
  27.3 1.1 %collective-permute-done.4 = f32[2,128]{1,0:T(2,128)S(1)} collective-permute-done((f32[2,128]{1,0:T(2,128)S(1)}, f32[2,128]{1,0:T(2,128)S(1)}, u32[]{:S(2)}, u32[]{:S(2)}) %collective-permute-start.4) | collective-permute-done | bytes 1056 | tf_op jit(solution)/shard_map/ppermute | solution.py:507
  28.4 0.6 %multiply_subtract_fusion = f32[2,128]{1,0:T(2,128)} fusion(f32[2,128]{1,0:T(2,128)S(1)} %collective-permute-done.4, f32[2,128]{1,0:T(2,128)S(1)} %get-tuple-element.13), kind=kLoop, calls=%fused_computation.4 | loop fusion | flops 2560 | bytes 3072 | tf_op jit(solution)/shard_map/sub | solution.py:510
  (3 shorter events, 0.0 us)
Async XLA Ops:
  1.4 6.3 %collective-permute-start = (f32[1,36,128]{2,1,0:T(8,128)S(1)}, f32[1,36,128]{2,1,0:T(8,128)S(1)}, u32[]{:S(2)}, u32[]{:S(2)}) collective-permute-start(f32[1,36,128]{2,1,0:T(8,128)S(1)} %maximum_bitcast_fusion), channel_id=1, source_target_pairs={{0,4},{1,5},{2,6},{3,7},{4,0},{5,1},{6,2},{7,3},{8,12},{9,13},{10,... | collective-permute-start | bytes 55304 | tf_op jit(solution)/shard_map/ppermute | solution.py:410
  7.7 4.6 %collective-permute-start.1 = (f32[2,36,128]{2,1,0:T(8,128)S(1)}, f32[2,36,128]{2,1,0:T(8,128)S(1)}, u32[]{:S(2)}, u32[]{:S(2)}) collective-permute-start(f32[2,36,128]{2,1,0:T(8,128)S(1)} %pad_maximum_fusion.2.z_ref), channel_id=1, source_target_pairs={{0,2},{1,3},{2,0},{3,1},{4,6},{5,7},{6,4},{7,5},{8,10},{9,11},{10,... | collective-permute-start | bytes 110600 | tf_op jit(solution)/shard_map/ppermute | solution.py:410
  12.3 4.5 %collective-permute-start.2 = (f32[4,36,128]{2,1,0:T(8,128)S(1)}, f32[4,36,128]{2,1,0:T(8,128)S(1)}, u32[]{:S(2)}, u32[]{:S(2)}) collective-permute-start(f32[4,36,128]{2,1,0:T(8,128)S(1)} %pad_maximum_fusion.1), channel_id=1, source_target_pairs={{0,1},{1,0},{2,3},{3,2},{4,5},{5,4},{6,7},{7,6},{8,9},{9,8},{10,11... | collective-permute-start | bytes 221192 | tf_op jit(solution)/shard_map/ppermute | solution.py:410
  21.4 4.3 %collective-permute-start.3 = (f32[2,8192]{1,0:T(2,128)S(1)}, f32[2,8192]{1,0:T(2,128)S(1)}, u32[]{:S(2)}, u32[]{:S(2)}) collective-permute-start(f32[2,8192]{1,0:T(2,128)S(1)} %shard_map.62.lse_ref.refs_0_), channel_id=1, source_target_pairs={{0,1},{1,0},{2,3},{3,2},{4,5},{5,4},{6,7},{7,6},{8,9},{9,8},{10,11... | collective-permute-start | bytes 196616 | tf_op jit(solution)/shard_map/ppermute | solution.py:410
  27.2 1.2 %collective-permute-start.4 = (f32[2,128]{1,0:T(2,128)S(1)}, f32[2,128]{1,0:T(2,128)S(1)}, u32[]{:S(2)}, u32[]{:S(2)}) collective-permute-start(f32[2,128]{1,0:T(2,128)S(1)} %get-tuple-element.13), channel_id=1, source_target_pairs={{0,8},{8,0},{1,9},{9,1},{2,10},{10,2},{3,11},{11,3},{4,12},{12,4},... | collective-permute-start | bytes 3080 | tf_op jit(solution)/shard_map/ppermute | solution.py:507
